TPU v7x, 256 devices: a whole 4x4x8 slice. The times are simulated.
256 devices in a mesh: band: 16 (over x_lo, z), slab: 16 (over y, x_hi, core).
Axes of the slice: x: 4 (x_hi: 2, x_lo: 2; x = x_hi * 2 + x_lo), y: 4, z: 8, core: 2. Of those that a mesh axis runs over, the one named last changes fastest.
Arguments:
- orbitals: float32 [256, 48, 2304], P('band', 'slab'), may hold values from -6 to 6
- partners: int32 [16, 2], replicated, may hold values from 0 to 15, as said below
- counts: int32 [16, 2], replicated, may hold values from 1 to 16
Outputs:
- forces: float32 [256, 48, 2304], P('band', 'slab')
- energy: float32 [], replicated
Inputs may be any that keep to these rules, and one draw needn't show every extreme that they name: `partners`: row g names two different band groups, neither of them g.
All inputs are finite; a program needn't handle non-finite values.
Results may differ from a plain program's by a relative error of at most 0.0001.
Values sent between devices are 32-bit elements; how exact they have to be, the bound alone decides.
A program may use at most 64 MiB of HBM per device.

v0:
```python
import functools
import math

import jax
import jax.numpy as jnp
from jax import lax
from jax.sharding import Mesh
from jax.sharding import PartitionSpec as P

NX = 48
NY = 48
NZ = 48
NZP = 96
BAND = ("band_0", "band_1")
SLAB = ("slab_0", "slab_1", "slab_2")
BAND_SLAB = ("band_0", "band_1", "slab_0", "slab_1", "slab_2")


slater_coeff = -((3.0 / math.pi) ** (1.0 / 3.0))
exchange_mix = 0.25
screening = 0.25
highest = lax.Precision.HIGHEST


def over_axes(value, axes):
    return functools.reduce(lax.psum, axes, value)


def dft_block(count_in, count_out, length, sign):
    row_iota = lax.broadcasted_iota(jnp.int32, (count_in, count_out), 0)
    col_iota = lax.broadcasted_iota(jnp.int32, (count_in, count_out), 1)
    phase_angle = 2.0 * math.pi / length * (row_iota * col_iota % length).astype(jnp.float32)
    cosine = jnp.cos(phase_angle)
    sine = jnp.sin(phase_angle)
    upper = jnp.stack([cosine, -sign * sine])
    lower = jnp.stack([sign * sine, cosine])
    return jnp.stack([upper, lower])


def wavenumber_sq(length):
    position = jnp.arange(length, dtype=jnp.int32)
    signed = jnp.where(position > length // 2, position - length, position).astype(jnp.float32)
    wave_number = 2.0 * math.pi / length * signed
    return wave_number * wave_number


def screened_potential(fields):
    spectrum = jnp.einsum(
        "coxyz,cdzk->doxyk", fields, dft_block(NZ, NZP, NZP, 1.0), precision=highest
    )
    spectrum = jnp.einsum(
        "coxyk,cdyq->doxqk", spectrum, dft_block(NY, NY, NY, 1.0), precision=highest
    )
    spectrum = jnp.einsum(
        "coxqk,cdxp->dopqk", spectrum, dft_block(NX, NX, NX, 1.0), precision=highest
    )
    total = (
        wavenumber_sq(NX)[:, None, None]
        + wavenumber_sq(NY)[None, :, None]
        + wavenumber_sq(NZP)[None, None, :]
    )
    kernel_table = 4.0 * math.pi / (NX * NY * NZP) / (total + screening * screening)
    spectrum = spectrum * kernel_table
    spectrum = jnp.einsum(
        "copqk,cdpx->doxqk", spectrum, dft_block(NX, NX, NX, -1.0), precision=highest
    )
    spectrum = jnp.einsum(
        "coxqk,cdqy->doxyk", spectrum, dft_block(NY, NY, NY, -1.0), precision=highest
    )
    return jnp.einsum(
        "coxyk,cdkz->doxyz", spectrum, dft_block(NZP, NZ, NZP, -1.0), precision=highest
    )


def pair_terms(own_orbs, visitors, active):
    per_device = own_orbs.shape[0]
    pair_density = own_orbs[None] * visitors * active[:, :, None, None]
    shaped = pair_density.reshape(2, per_device, NX, NY, NZ)
    fields = screened_potential(shaped).reshape(pair_density.shape)
    own_force = -exchange_mix * jnp.sum(fields * visitors, axis=0)
    partner_force = -exchange_mix * fields * own_orbs[None]
    energy_term = jnp.sum(pair_density * fields)
    return (own_force, partner_force, energy_term)


def request_rows(held_rows, partners, width):
    row_index = (partners[:, :, None] * width + jnp.arange(width, dtype=jnp.int32)).reshape(-1)
    return jnp.take(held_rows, row_index, axis=0)


def return_rows(pieces, partners, bands):
    flat = pieces.reshape(bands * 2, -1)
    targets = jnp.arange(bands, dtype=jnp.int32)[:, None]
    onehot = (partners.reshape(-1)[None, :] == targets).astype(jnp.float32)
    summed = jnp.dot(onehot, flat, precision=highest)
    width = pieces.shape[0] // (bands * 2)
    return summed.reshape((bands * width,) + pieces.shape[1:])


def body(orbitals, partners, counts):
    bands = lax.axis_size(BAND)
    slabs = lax.axis_size(SLAB)
    band_index = lax.axis_index(BAND)
    slab_index = lax.axis_index(SLAB)
    orb_group = orbitals.shape[0]
    per_device = orb_group // slabs
    total_orbs = orb_group * bands
    squares = jnp.sum(orbitals * orbitals, axis=0)
    density = 2.0 / total_orbs * over_axes(squares, BAND)
    local_pot = slater_coeff * jnp.cbrt(density)
    band_match = jnp.arange(bands, dtype=jnp.int32)[:, None] == band_index
    my_counts = jnp.sum(jnp.where(band_match, counts, 0), axis=0)
    local_rows = slab_index * per_device + jnp.arange(per_device, dtype=jnp.int32)
    active = (local_rows[None, :] < my_counts[:, None]).astype(jnp.float32)
    own_orbs = lax.all_to_all(orbitals, SLAB, split_axis=0, concat_axis=1, tiled=True)
    held_rows = lax.all_to_all(own_orbs, BAND, split_axis=1, concat_axis=0, tiled=True)
    wanted = request_rows(held_rows, partners, per_device)
    visitors = lax.all_to_all(wanted, BAND, split_axis=0, concat_axis=1, tiled=True)
    visitors = visitors.reshape((2, per_device) + own_orbs.shape[1:])
    own_force, partner_force, energy_term = pair_terms(own_orbs, visitors, active)
    outgoing = partner_force.reshape((2 * per_device,) + own_orbs.shape[1:])
    outgoing = lax.all_to_all(outgoing, BAND, split_axis=1, concat_axis=0, tiled=True)
    returned = lax.all_to_all(
        return_rows(outgoing, partners, bands), BAND, split_axis=0, concat_axis=1, tiled=True
    )
    exchange_force = lax.all_to_all(
        own_force + returned, SLAB, split_axis=1, concat_axis=0, tiled=True
    )
    energy_total = over_axes(energy_term, BAND_SLAB)
    energy = -energy_total / (2.0 * total_orbs * NX * NY * NZ)
    forces = local_pot[None] * orbitals + exchange_force
    return (forces, energy)


def solution(mesh):
    torus = Mesh(
        mesh.devices.reshape(2, 8, 4, 2, 2), ("band_0", "band_1", "slab_0", "slab_1", "slab_2")
    )
    in_specs = (P(BAND, SLAB, None), P(), P())
    out_specs = (P(BAND, SLAB, None), P())
    return jax.shard_map(body, mesh=torus, in_specs=in_specs, out_specs=out_specs, check_vma=False)
```

profile of v0, /device:TPU:1, one launch (start us, length us, event | category | flops | bytes accessed | tf_op | source)
XLA Modules:
  0.0 241.4 jit_solution(8340046165394980093)
XLA Ops:
  0.6 2.1 copy.93
  2.8 8.4 %all-to-all-start = ((f32[16,3,2304]{2,1,0:T(4,128)}), f32[16,3,2304]{2,1,0:T(4,128)S(1)}, u32[]{:S(2)}, u32[]{:S(2)}) async-start(f32[16,3,2304]{2,1,0:T(4,128)} %copy.93), calls=%async_computation | async-start | bytes 1179648 | tf_op jit(solution)/shard_map/all_to_all | solution.py:115
  11.2 0.8 copy.98
  12.1 0.8 select_reduce_fusion
  13.1 9.9 %all-to-all-done = f32[16,3,2304]{2,1,0:T(4,128)S(1)} async-done(((f32[16,3,2304]{2,1,0:T(4,128)}), f32[16,3,2304]{2,1,0:T(4,128)S(1)}, u32[]{:S(2)}, u32[]{:S(2)}) %all-to-all-start) | async-done | bytes 442400 | tf_op jit(solution)/shard_map/all_to_all | solution.py:115
  23.1 1.4 all_to_all.72
  24.4 8.4 %all-to-all-start.1 = ((f32[1,48,2304]{2,0,1:T(1,128)}), f32[1,48,2304]{2,0,1:T(1,128)S(1)}, u32[]{:S(2)}, u32[]{:S(2)}) async-start(f32[1,48,2304]{2,0,1:T(1,128)} %all_to_all.72), calls=%async_computation.1 | async-start | bytes 884736 | tf_op jit(solution)/shard_map/all_to_all | solution.py:116
  33.4 0.6 maximum_bitcast_fusion.10
  34.1 10.5 %all-to-all-done.1 = f32[1,48,2304]{2,0,1:T(1,128)S(1)} async-done(((f32[1,48,2304]{2,0,1:T(1,128)}), f32[1,48,2304]{2,0,1:T(1,128)S(1)}, u32[]{:S(2)}, u32[]{:S(2)}) %all-to-all-start.1) | async-done | bytes 442400 | tf_op jit(solution)/shard_map/all_to_all | solution.py:116
  44.5 1.0 reduce.3
  45.8 1.3 gather_fusion
  47.0 1.3 broadcast_select_fusion
  48.4 5.8 %all-to-all-start.2 = ((f32[32,3,2304]{2,1,0:T(4,128)}), f32[32,3,2304]{2,1,0:T(4,128)S(1)}, u32[]{:S(2)}, u32[]{:S(2)}) async-start(f32[32,3,2304]{2,1,0:T(4,128)} %broadcast_select_fusion), calls=%async_computation.2 | async-start | bytes 2359296 | tf_op jit(solution)/shard_map/all_to_all | solution.py:118
  54.2 0.6 maximum_bitcast_fusion.8
  54.9 0.7 fusion.49
  55.7 1.4 add_divide_fusion
  57.1 0.8 mul.413
  57.9 1.4 copy.119
  59.5 1.0 mul.434
  60.4 21.4 %all-to-all-done.2 = f32[32,3,2304]{2,1,0:T(4,128)S(1)} async-done(((f32[32,3,2304]{2,1,0:T(4,128)}), f32[32,3,2304]{2,1,0:T(4,128)S(1)}, u32[]{:S(2)}, u32[]{:S(2)}) %all-to-all-start.2) | async-done | bytes 884768 | tf_op jit(solution)/shard_map/all_to_all | solution.py:118
  81.8 1.4 copy.189
  83.2 2.7 %reshape.398 = f32[2,48,48,48]{3,2,0,1:T(8,128)S(1)} reshape(f32[2,16,3,2304]{3,0,2,1:T(2,128)} %bitcast.149) | data formatting | bytes 1769472 | tf_op jit(solution)/shard_map/reshape | solution.py:119
  85.9 3.6 %reshape.402 = f32[2,1,48,48,48]{4,3,0,2,1:T(8,128)} reshape(f32[2,16,3,2304]{3,0,2,1:T(2,128)} %bitcast.150) | data formatting | bytes 1769472 | tf_op jit(solution)/shard_map/reshape | solution.py:119
  89.6 3.0 %fusion.19 = f32[2,48,48,96]{3,2,1,0:T(8,128)S(1)} fusion(f32[2,48,48,48]{3,2,0,1:T(8,128)S(1)} %reshape.398, f32[2]{0:T(128)S(1)} %compare_convert_fusion, f32[48,48,48]{2,1,0:T(8,128)S(1)} %mul.413, f32[1,2,48,96]{3,2,0,1:T(8,128)} %get-tuple-element.25, f32[1,2,48,96]{3,2,0,1:T(8,128)} %get-tuple-element.24), kind=kOutput, calls=%fused_computation.23 | convolution fusion | flops 510068736 | bytes 3170312 | tf_op jit(solution)/shard_map/coxyz,cdzk->doxyk/dot_general | solution.py:48
  92.7 2.2 fusion.22
  94.9 2.7 %bitcast_multiply_fusion = f32[2,48,48,96]{3,1,2,0:T(8,128)S(1)} fusion(f32[2,48,48,96]{3,2,1,0:T(8,128)S(1)} %fusion.22, f32[48,48,96]{2,0,1:T(8,128)S(1)} %copy-done, f32[1,2,48,48]{2,3,0,1:T(8,128)S(1)} %copy-done.5, f32[1,2,48,48]{2,3,0,1:T(8,128)S(1)} %copy-done.6), kind=kOutput, calls=%fused_computation.7 | convolution fusion | flops 510059520 | bytes 4460544 | tf_op jit(solution)/shard_map/coxqk,cdxp->dopqk/dot_general | solution.py:54
  97.7 2.2 fusion.27
  99.9 2.7 %fusion.30 = f32[2,48,48,96]{3,2,1,0:T(8,128)S(1)} fusion(f32[2,48,48,96]{3,1,2,0:T(8,128)S(1)} %fusion.27, f32[1,2,48,48]{2,3,1,0:T(8,128)S(1)} %copy-done.4, f32[1,2,48,48]{2,3,1,0:T(8,128)S(1)} %copy-done.3), kind=kOutput, calls=%fused_computation.26 | convolution fusion | flops 509617152 | bytes 3575808 | tf_op jit(solution)/shard_map/coxqk,cdqy->doxyk/dot_general | solution.py:67
  102.6 3.0 %copy.111 = f32[2,1,48,48,48]{3,4,2,0,1:T(8,128)} copy(f32[2,1,48,48,48]{4,3,0,2,1:T(8,128)} %reshape.402) | data formatting | bytes 1769472 | tf_op jit(solution)/shard_map/reshape | solution.py:119
  105.6 8.1 %multiply_reduce_fusion = (f32[]{:T(128)}, f32[48,48,48]{1,2,0:T(8,128)S(1)}, f32[2,1,48,48,48]{3,4,2,0,1:T(8,128)}) fusion(f32[2,1,48,48,48]{3,4,2,0,1:T(8,128)} %copy.111, f32[2]{0:T(128)S(1)} %compare_convert_fusion, f32[48,48,48]{1,2,0:T(8,128)} %copy.119, f32[2,48,48,96]{3,2,1,0:T(8,128)S(1)} %fusion.30, f32[1,2,96,48]{2,3,0,1:T(8,128)} %get-tuple-element.21, ...), kind=kOutput, calls=%fused_computation.19 | convolution fusion | flops 510842880 | bytes 4497420 | tf_op jit(solution)/shard_map/coxyk,cdkz->doxyz/dot_general | solution.py:70
  113.8 2.0 copy.113
  115.8 1.9 reshape.403
  117.7 1.4 broadcast_multiply_fusion.1
  119.1 0.7 copy.114
  119.8 28.6 %all_to_all.79 = f32[2,48,2304]{2,0,1:T(2,128)S(1)} all-to-all(f32[2,48,2304]{2,0,1:T(2,128)S(1)} %copy.114), channel_id=1, replica_groups=mesh['band_0'=2,'band_1'=8,'slab_0'=4,'slab_1'=2,'slab_2'=2] {'band_0','..., dimensions={1} | all-to-all | bytes 1769472 | tf_op jit(solution)/shard_map/all_to_all | solution.py:122
  149.2 1.1 copy.117
  150.3 5.7 %all-to-all-start.4 = ((f32[16,3,2304]{2,1,0:T(4,128)}), f32[16,3,2304]{2,1,0:T(4,128)}, u32[]{:S(2)}, u32[]{:S(2)}) async-start(f32[16,3,2304]{2,1,0:T(4,128)} %copy.117), calls=%async_computation.4 | async-start | bytes 1179648 | tf_op jit(solution)/shard_map/all_to_all | solution.py:123
  156.1 9.3 %all-reduce.1 = (f32[3,2304]{1,0:T(4,128)S(1)}, f32[]{:T(128)}) all-reduce(f32[3,2304]{1,0:T(4,128)S(1)} %multiply_reduce_fusion.2, f32[]{:T(128)} %get-tuple-element.10), channel_id=1, replica_groups=mesh['band_0'=2,'band_1'=8,'slab_0'=4,'slab_1'=2,'slab_2'=2] {'band_0'}, use_global_device_ids=true, to_apply=%region_1.0 | all-reduce | flops 6913 | bytes 55304 | tf_op jit(solution)/shard_map/psum | solution.py:26
  165.4 24.0 %all-reduce = (f32[3,2304]{1,0:T(4,128)}, f32[]{:T(128)}) all-reduce(f32[3,2304]{1,0:T(4,128)S(1)} %get-tuple-element.14, f32[]{:T(128)} %get-tuple-element.15), channel_id=1, replica_groups=mesh['band_0'=2,'band_1'=8,'slab_0'=4,'slab_1'=2,'slab_2'=2] {'band_1'}, use_global_device_ids=true, to_apply=%region_2.0 | all-reduce | flops 6913 | bytes 55304 | tf_op jit(solution)/shard_map/psum | solution.py:26
  189.4 7.1 %psum.53 = f32[]{:T(128)} all-reduce(f32[]{:T(128)} %get-tuple-element.13), channel_id=1, replica_groups=mesh['band_0'=2,'band_1'=8,'slab_0'=4,'slab_1'=2,'slab_2'=2] {'slab_0'}, use_global_device_ids=true, to_apply=%region_8.9 | all-reduce | flops 1 | bytes 8 | tf_op jit(solution)/shard_map/psum | solution.py:26
  196.5 5.9 %psum.54 = f32[]{:T(128)} all-reduce(f32[]{:T(128)} %psum.53), channel_id=1, replica_groups=mesh['band_0'=2,'band_1'=8,'slab_0'=4,'slab_1'=2,'slab_2'=2] {'slab_1'}, use_global_device_ids=true, to_apply=%region_9.10 | all-reduce | flops 1 | bytes 8 | tf_op jit(solution)/shard_map/psum | solution.py:26
  202.4 15.8 %psum.55 = f32[]{:T(128)} all-reduce(f32[]{:T(128)} %psum.54), channel_id=1, replica_groups=mesh['band_0'=2,'band_1'=8,'slab_0'=4,'slab_1'=2,'slab_2'=2] {'slab_2'}, use_global_device_ids=true, to_apply=%region_10.11 | all-reduce | flops 1 | bytes 8 | tf_op jit(solution)/shard_map/psum | solution.py:26
  219.8 1.3 all_to_all.69
  221.2 1.2 copy.118
  222.4 5.1 %all-to-all-start.5 = ((f32[1,48,2304]{2,0,1:T(1,128)}), f32[1,48,2304]{2,0,1:T(1,128)S(1)}, u32[]{:S(2)}, u32[]{:S(2)}) async-start(f32[1,48,2304]{2,0,1:T(1,128)} %copy.118), calls=%async_computation.5 | async-start | bytes 884736 | tf_op jit(solution)/shard_map/all_to_all | solution.py:126
  227.6 10.2 %all-to-all-done.5 = f32[1,48,2304]{2,0,1:T(1,128)S(1)} async-done(((f32[1,48,2304]{2,0,1:T(1,128)}), f32[1,48,2304]{2,0,1:T(1,128)S(1)}, u32[]{:S(2)}, u32[]{:S(2)}) %all-to-all-start.5) | async-done | bytes 442400 | tf_op jit(solution)/shard_map/all_to_all | solution.py:126
  237.8 1.0 reduce.4
  239.4 0.8 copy.121
  (45 shorter events, 3.8 us)
Async XLA Ops:
  2.8 20.3 %all-to-all-start = ((f32[16,3,2304]{2,1,0:T(4,128)}), f32[16,3,2304]{2,1,0:T(4,128)S(1)}, u32[]{:S(2)}, u32[]{:S(2)}) async-start(f32[16,3,2304]{2,1,0:T(4,128)} %copy.93), calls=%async_computation | async-start | bytes 1179648 | tf_op jit(solution)/shard_map/all_to_all | solution.py:115
  24.4 20.1 %all-to-all-start.1 = ((f32[1,48,2304]{2,0,1:T(1,128)}), f32[1,48,2304]{2,0,1:T(1,128)S(1)}, u32[]{:S(2)}, u32[]{:S(2)}) async-start(f32[1,48,2304]{2,0,1:T(1,128)} %all_to_all.72), calls=%async_computation.1 | async-start | bytes 884736 | tf_op jit(solution)/shard_map/all_to_all | solution.py:116
  48.4 33.5 %all-to-all-start.2 = ((f32[32,3,2304]{2,1,0:T(4,128)}), f32[32,3,2304]{2,1,0:T(4,128)S(1)}, u32[]{:S(2)}, u32[]{:S(2)}) async-start(f32[32,3,2304]{2,1,0:T(4,128)} %broadcast_select_fusion), calls=%async_computation.2 | async-start | bytes 2359296 | tf_op jit(solution)/shard_map/all_to_all | solution.py:118
  89.6 3.1 %copy-start.5 = (f32[1,2,48,48]{2,3,0,1:T(8,128)S(1)}, f32[1,2,48,48]{2,3,0,1:T(8,128)}, u32[]{:S(2)}) copy-start(f32[1,2,48,48]{2,3,0,1:T(8,128)} %get-tuple-element.17) | copy-start | bytes 55300
  89.6 3.1 %copy-start.6 = (f32[1,2,48,48]{2,3,0,1:T(8,128)S(1)}, f32[1,2,48,48]{2,3,0,1:T(8,128)}, u32[]{:S(2)}) copy-start(f32[1,2,48,48]{2,3,0,1:T(8,128)} %get-tuple-element.22) | copy-start | bytes 55300
  92.7 2.2 copy-start
  94.9 2.8 %copy-start.3 = (f32[1,2,48,48]{2,3,1,0:T(8,128)S(1)}, f32[1,2,48,48]{2,3,1,0:T(8,128)}, u32[]{:S(2)}) copy-start(f32[1,2,48,48]{2,3,1,0:T(8,128)} %get-tuple-element.16) | copy-start | bytes 55300
  94.9 2.8 %copy-start.4 = (f32[1,2,48,48]{2,3,1,0:T(8,128)S(1)}, f32[1,2,48,48]{2,3,1,0:T(8,128)}, u32[]{:S(2)}) copy-start(f32[1,2,48,48]{2,3,1,0:T(8,128)} %get-tuple-element.23) | copy-start | bytes 55300
  148.4 7.6 %copy-start.1 = (f32[16,3,2304]{2,0,1:T(8,128)S(1)}, f32[16,3,2304]{2,0,1:T(8,128)}, u32[]{:S(2)}) copy-start(f32[16,3,2304]{2,0,1:T(8,128)} %param.3) | copy-start | bytes 1327108
  150.3 69.5 %all-to-all-start.4 = ((f32[16,3,2304]{2,1,0:T(4,128)}), f32[16,3,2304]{2,1,0:T(4,128)}, u32[]{:S(2)}, u32[]{:S(2)}) async-start(f32[16,3,2304]{2,1,0:T(4,128)} %copy.117), calls=%async_computation.4 | async-start | bytes 1179648 | tf_op jit(solution)/shard_map/all_to_all | solution.py:123
  219.2 8.4 %copy-start.7 = (f32[3,2304]{1,0:T(4,128)S(1)}, f32[3,2304]{1,0:T(4,128)}, u32[]{:S(2)}) copy-start(f32[3,2304]{1,0:T(4,128)} %get-tuple-element.12) | copy-start | bytes 82948
  221.1 17.9 %copy-start.2 = (f32[16,3,2304]{2,0,1:T(8,128)S(1)}, f32[16,3,2304]{2,0,1:T(8,128)}, u32[]{:S(2)}) copy-start(f32[16,3,2304]{2,0,1:T(8,128)} %param.3) | copy-start | bytes 1327108
  222.4 15.4 %all-to-all-start.5 = ((f32[1,48,2304]{2,0,1:T(1,128)}), f32[1,48,2304]{2,0,1:T(1,128)S(1)}, u32[]{:S(2)}, u32[]{:S(2)}) async-start(f32[1,48,2304]{2,0,1:T(1,128)} %copy.118), calls=%async_computation.5 | async-start | bytes 884736 | tf_op jit(solution)/shard_map/all_to_all | solution.py:126
where the time goes:
time: 242 us; the launch traced here: 241 us
  blocking collectives  90.7 us (37%)
  waiting for transfers between devices  52 us (21%)
  starting transfers between devices  33.5 us (14%)
  local copies, waits for them, and re-layouts  30.4 us (13%)
  matrix products  21.5 us (9%)
  other arithmetic  10.6 us (4%)
  between operations  2.8 us (1%)
    psum x5, blocking collectives, over_axes(): return functools.reduce(lax.psum, axes, value)  62.1 us
    all_to_all x1, blocking collectives, body(): lax.all_to_all(outgoing, BAND, split_axis=1, concat_axis=0, tiled=True)  28.6 us
    all_to_all x1, waiting for transfers between devices, body(): lax.all_to_all(wanted, BAND, split_axis=0, concat_axis=1, tiled=True)  21.4 us
    all_to_all x1, waiting for transfers between devices, body(): lax.all_to_all(own_orbs, BAND, split_axis=1, concat_axis=0, tiled=True)  10.5 us
    all_to_all x1, waiting for transfers between devices, body(): lax.all_to_all(own_force + returned, SLAB, split_axis=1, concat_axis=0, t...  10.2 us
    all_to_all x1, waiting for transfers between devices, body(): lax.all_to_all(orbitals, SLAB, split_axis=0, concat_axis=1, tiled=True)  9.94 us
    reshape x3, local copies, waits for them, and re-layouts, body(): visitors = visitors.reshape((2, per_device) + own_orbs.shape[1:])  9.42 us
    all_to_all x1, starting transfers between devices, body(): lax.all_to_all(orbitals, SLAB, split_axis=0, concat_axis=1, tiled=True)  8.44 us
  transfers between devices with their start and end apart: 5, of which 4 were waited for; matrix products, arithmetic and copies ran while one was open for 4% of the time, Pallas kernels for 0%

commit v1 on v0

v1 whole, which is shorter than its diff:
```python
import functools
import math

import jax
import jax.numpy as jnp
import numpy as np
from jax import lax
from jax.experimental import pallas as pl
from jax.experimental.pallas import tpu as pltpu
from jax.sharding import PartitionSpec as P

NX = 48
NY = 48
NZ = 48
NZP = 96
N = 16
ROWS = 54
BLK = 56
LANES = 128
PAIRS = 2 * N
SLATER = -((3.0 / math.pi) ** (1.0 / 3.0))
MIX = 0.25
SCREENING = 0.25
F32 = jnp.float32
BF16 = jnp.bfloat16
MESH = pl.DeviceIdType.MESH


def split_np(w):
    hi = w.astype(np.float32).astype(jnp.bfloat16)
    lo = (w - hi.astype(np.float64)).astype(np.float32).astype(jnp.bfloat16)
    return hi, lo


def cas(length):
    j = np.arange(length)
    angle = 2.0 * np.pi * ((j[:, None] * j[None, :]) % length) / length
    return (np.cos(angle) + np.sin(angle)) / np.sqrt(length)


def constants():
    h = cas(48)
    order = np.array([3 * p + plane for plane in range(3) for p in range(16)])
    wx = h[:, order]

    def left(w):
        hi, lo = split_np(w)
        return np.concatenate([hi, hi, lo], axis=1)

    small = np.stack([left(wx), left(h), left(wx.T)])
    hz = cas(NZP)[:NZ, :]
    full = np.zeros((384, 8, LANES))
    for y8 in range(8):
        full[y8 * 48 : (y8 + 1) * 48, y8, :NZP] = hz
    full = full.reshape(384, 8 * LANES)
    fwd = np.concatenate(
        [full[0:128, 0:256], full[0:256, 256:512], full[128:384, 512:768], full[256:384, 768:1024]]
    )
    back = full.T
    inv01 = back[0 : 6 * 128, 0:256]
    inv2 = back[5 * 128 : 8 * 128, 256:384]
    return small, np.concatenate(split_np(fwd)), np.concatenate(split_np(inv01)), np.concatenate(split_np(inv2))


def split(x):
    hi = x.astype(BF16)
    lo = (x - hi.astype(F32)).astype(BF16)
    return hi, lo


def dot(a, b):
    return jnp.dot(a, b, preferred_element_type=F32)


def dot3(x_hl, w_hi, w_lo, m):
    both = dot(x_hl, w_hi)
    return both[:m] + both[m:] + dot(x_hl[:m], w_lo)


def left3(w3, x):
    hi, lo = split(x)
    return dot(w3, jnp.concatenate([hi, lo, hi], axis=0))


def fill_table(table):
    def wave_sq(index, length):
        signed = jnp.where(index > length // 2, index - length, index).astype(F32)
        wave = 2.0 * math.pi / length * signed
        return wave * wave

    lane = lax.broadcasted_iota(jnp.int32, (48, LANES), 1)
    row = lax.broadcasted_iota(jnp.int32, (48, LANES), 0)
    yz = wave_sq(row, NY) + wave_sq(lane, NZP) + SCREENING * SCREENING

    def step(qx, carry):
        wx = wave_sq(jnp.full((48, LANES), qx, jnp.int32), NX)
        value = jnp.where(lane < NZP, 4.0 * math.pi / (yz + wx), 0.0)
        table[pl.ds(pl.multiple_of(qx * 48, 8), 48), :] = value
        return carry

    lax.fori_loop(0, 48, step, 0)


def convolve(pd, pot, base, work, table, small, fwd, inv01, inv2):
    rows = 288

    def gather(ref, t):
        tiles = [
            ref[pl.ds(base + plane * 18 + yg * 3 + t, 16, stride=BLK), :]
            for yg in range(6)
            for plane in range(3)
        ]
        return jnp.concatenate(tiles, axis=0)

    def scatter_z(j, value):
        for yg in range(6):
            for half in range(2):
                y = yg * 8 + 2 * j + half
                work[pl.ds(y * 48, 48), :] = value[
                    yg * 48 : (yg + 1) * 48, half * LANES : (half + 1) * LANES
                ]

    def stack(t):
        hi, lo = split(gather(pd, t))
        return jnp.concatenate([hi, lo], axis=0)

    s0 = stack(0)
    scatter_z(0, dot3(s0, fwd[0:128], fwd[768 : 768 + 128], rows))
    s1 = stack(1)
    s01 = jnp.concatenate([s0, s1], axis=1)
    scatter_z(1, dot3(s01, fwd[128:384], fwd[768 + 128 : 768 + 384], rows))
    s2 = stack(2)
    s12 = jnp.concatenate([s1, s2], axis=1)
    scatter_z(2, dot3(s12, fwd[384:640], fwd[768 + 384 : 768 + 640], rows))
    scatter_z(3, dot3(s2, fwd[640:768], fwd[768 + 640 : 768 + 768], rows))

    def along_x(which):
        w3 = small[which]

        def step(i, carry):
            start = pl.multiple_of(i * 384, 8)
            block = work[pl.ds(start, 384), :]
            wide = jnp.concatenate([block[48 * u : 48 * (u + 1)] for u in range(8)], axis=1)
            out = left3(w3, wide)
            work[pl.ds(start, 384), :] = jnp.concatenate(
                [out[:, LANES * u : LANES * (u + 1)] for u in range(8)], axis=0
            )
            return carry

        lax.fori_loop(0, 6, step, 0)

    along_x(0)
    wy3 = small[1]

    def y_step(i, carry):
        qx = i * 8
        wide = jnp.concatenate(
            [work[pl.ds(qx + u, 48, stride=48), :] for u in range(8)], axis=1
        )
        spectrum = left3(wy3, wide)
        k = table[pl.ds(pl.multiple_of(qx * 48, 8), 384), :]
        k = jnp.concatenate([k[48 * u : 48 * (u + 1)] for u in range(8)], axis=1)
        out = left3(wy3, spectrum * k)
        for u in range(8):
            work[pl.ds(qx + u, 48, stride=48), :] = out[:, LANES * u : LANES * (u + 1)]
        return carry

    lax.fori_loop(0, 6, y_step, 0)
    along_x(2)

    def gather_y8(y8):
        tiles = [work[pl.ds((yg * 8 + y8) * 48, 48), :] for yg in range(6)]
        hi, lo = split(jnp.concatenate(tiles, axis=0))
        return jnp.concatenate([hi, lo], axis=0)

    energy = jnp.zeros((16, LANES), F32)

    def scatter_t(t, value, energy):
        for yg in range(6):
            for plane in range(3):
                at = pl.ds(base + plane * 18 + yg * 3 + t, 16, stride=BLK)
                tile = value[(yg * 3 + plane) * 16 : (yg * 3 + plane + 1) * 16]
                pot[at, :] = tile
                energy = energy + tile * pd[at, :]
        return energy

    parts = [gather_y8(y8) for y8 in range(6)]
    first = jnp.concatenate(parts, axis=1)
    out = dot3(first, inv01[0:768], inv01[768:1536], rows)
    energy = scatter_t(0, out[:, 0:128], energy)
    energy = scatter_t(1, out[:, 128:256], energy)
    second = jnp.concatenate([parts[5], gather_y8(6), gather_y8(7)], axis=1)
    energy = scatter_t(2, dot3(second, inv2[0:384], inv2[384:768], rows), energy)
    total = jnp.sum(energy, axis=0, keepdims=True)
    pot[pl.ds(base + ROWS, 16, stride=BLK), :] = jnp.broadcast_to(total, (16, LANES))


def block(index):
    return pl.ds(pl.multiple_of(index * BLK, 8), BLK)


def slot(ref, index):
    return ref.at[index] if len(ref.shape) == 3 else ref.at[block(index)]


def kernel(
    orb, partners, counts, small, fwd_hbm, inv01_hbm, inv2_hbm,
    forces, energy_out,
    src, held, pairs, tasks, pots, back, partial, final, ret, dens, dens_in, local, work, table, fwd, inv01, inv2,
    const_sems, sa, ra, sb, rb, sc, rc, sd, rd, sn, rn,
):
    band = lax.axis_index("band")
    slab = lax.axis_index("slab")

    def peer(me, i):
        return lax.rem(me + i, N)

    def each_peer(fn):
        def step(i, carry):
            fn(i)
            return carry

        lax.fori_loop(1, N, step, 0)

    barrier = pltpu.get_barrier_semaphore()

    def greet(i):
        pl.semaphore_signal(barrier, inc=1, device_id={"band": peer(band, i)}, device_id_type=MESH)
        pl.semaphore_signal(barrier, inc=1, device_id={"slab": peer(slab, i)}, device_id_type=MESH)

    each_peer(greet)
    loads = [
        pltpu.make_async_copy(a, b, const_sems.at[i])
        for i, (a, b) in enumerate(((fwd_hbm, fwd), (inv01_hbm, inv01), (inv2_hbm, inv2)))
    ]
    for load in loads:
        load.start()

    for plane in range(3):
        for chunk in range(18):
            tile = orb[plane, :, chunk * LANES : (chunk + 1) * LANES]
            src[pl.ds(plane * 18 + chunk, N, stride=BLK), :] = tile
            dens[pl.ds(plane * 18 + chunk, 1), :] = jnp.sum(tile * tile, axis=0, keepdims=True)
    pl.semaphore_wait(barrier, 2 * (N - 1))

    def band_copy(a, b, at_peer, at_me, send, recv, i):
        p = peer(band, i)
        return pltpu.make_async_remote_copy(
            src_ref=a.at[block(p)] if at_peer else a,
            dst_ref=slot(b, at_me),
            send_sem=send.at[p],
            recv_sem=recv.at[at_me],
            device_id={"band": p},
            device_id_type=MESH,
        )

    def slab_copy(a, b, k, send, recv, i):
        p = peer(slab, i)
        return pltpu.make_async_remote_copy(
            src_ref=a.at[block(k * N + p)],
            dst_ref=b.at[block(k * N + slab)],
            send_sem=send.at[k * N + p],
            recv_sem=recv.at[k * N + slab],
            device_id={"slab": p},
            device_id_type=MESH,
        )

    def landed(b, k, at, recv, send, p):
        return pltpu.make_async_remote_copy(
            src_ref=slot(b, k * N + p),
            dst_ref=slot(b, k * N + p),
            send_sem=send.at[k * N + p],
            recv_sem=recv.at[k * N + p],
            device_id=at,
            device_id_type=MESH,
        )

    def wait_band(b, recv, send):
        each_peer(
            lambda i: landed(b, 0, {"band": peer(band, i)}, recv, send, peer(band, i)).wait_recv()
        )

    def wait_slab(b, k, recv, send):
        each_peer(
            lambda i: landed(b, k, {"slab": peer(slab, i)}, recv, send, peer(slab, i)).wait_recv()
        )

    each_peer(lambda i: band_copy(src, held, True, band, sa, ra, i).start())
    held[band] = src[block(band), :]
    each_peer(lambda i: band_copy(dens, dens_in, False, band, sn, rn, i).start())
    dens_in[block(band), :] = dens[...]

    fill_table(table)
    wait_band(held, ra, sa)

    for k in range(2):
        def pair(g, k=k):
            partner = partners[k, g]
            active = jnp.where(band < counts[k, g], 1.0, 0.0).astype(F32)
            return held[g] * held[partner] * active

        def send_pair(i, k=k):
            g = peer(slab, i)
            pairs[block(k * N + g), :] = pair(g)
            slab_copy(pairs, tasks, k, sb, rb, i).start()

        each_peer(send_pair)
        tasks[block(k * N + slab), :] = pair(slab)

    for load in loads:
        load.wait()

    for k in range(2):
        wait_slab(tasks, k, rb, sb)
        convolve(tasks, pots, k * N * BLK, work, table, small, fwd, inv01, inv2)
        each_peer(lambda i: slab_copy(pots, back, k, sc, rc, i).start())
        back[block(k * N + slab), :] = pots[block(k * N + slab), :]

    wait_band(dens_in, rn, sn)
    total = dens_in[pl.ds(0, BLK), :]
    for b in range(1, N):
        total = total + dens_in[pl.ds(b * BLK, BLK), :]
    total = total * (2.0 / (N * N))
    safe = jnp.maximum(total, 1e-37)
    root = jnp.exp(jnp.log(safe) * (1.0 / 3.0))
    root = root * (2.0 + safe / (root * root * root)) * (1.0 / 3.0)
    local[...] = SLATER * jnp.where(total > 0.0, root, 0.0)

    row = lax.broadcasted_iota(jnp.int32, (N, PAIRS), 0)
    col = lax.broadcasted_iota(jnp.int32, (N, PAIRS), 1)
    names = jnp.full((N, PAIRS), -1, jnp.int32)
    for k in range(2):
        for g in range(N):
            names = jnp.where(col == k * N + g, partners[k, g], names)
    onehot = jnp.where(names == row, 1.0, 0.0).astype(BF16)
    onehot3 = jnp.concatenate([onehot, onehot, onehot], axis=1)

    wait_slab(back, 0, rc, sc)
    wait_slab(back, 1, rc, sc)

    def own_terms(g, carry):
        phi = held[g]
        own = jnp.zeros((BLK, LANES), F32)
        for k in range(2):
            pot = back[block(k * N + g), :]
            own = own + pot * held[partners[k, g]]
            ret[block(k * N + g), :] = pot * phi
        partial[block(g), :] = own
        return carry

    lax.fori_loop(0, N, own_terms, 0)

    for first in range(0, ROWS, 9):
        wide = jnp.concatenate(
            [ret[pl.ds(first + u, PAIRS, stride=BLK), :] for u in range(9)], axis=1
        )
        hi, mid = split(wide)
        low = (wide - hi.astype(F32) - mid.astype(F32)).astype(BF16)
        summed = dot(onehot3, jnp.concatenate([hi, mid, low], axis=0))
        for u in range(9):
            at = pl.ds(first + u, N, stride=BLK)
            partial[at, :] = -MIX * (partial[at, :] + summed[:, u * LANES : (u + 1) * LANES])
    index_energy = jnp.sum(back[pl.ds(ROWS, PAIRS, stride=BLK), :], axis=0, keepdims=True)
    partial[pl.ds(ROWS, N, stride=BLK), :] = jnp.broadcast_to(index_energy, (N, LANES))

    each_peer(lambda i: band_copy(partial, final, True, band, sd, rd, i).start())
    final[block(band), :] = partial[block(band), :]
    wait_band(final, rd, sd)

    for plane in range(3):
        for chunk in range(18):
            r = plane * 18 + chunk
            lanes = slice(chunk * LANES, (chunk + 1) * LANES)
            forces[plane, :, lanes] = (
                local[pl.ds(r, 1), :] * orb[plane, :, lanes] + final[pl.ds(r, N, stride=BLK), :]
            )
    energies = final[pl.ds(ROWS, N, stride=BLK), :]
    energy_out[0, 0] = jnp.sum(energies) * (-1.0 / (2.0 * N * N * NX * NY * NZ))

    each_peer(lambda i: band_copy(src, held, True, band, sa, ra, i).wait_send())
    each_peer(lambda i: band_copy(dens, dens_in, False, band, sn, rn, i).wait_send())
    for k in range(2):
        each_peer(lambda i: slab_copy(pairs, tasks, k, sb, rb, i).wait_send())
        each_peer(lambda i: slab_copy(pots, back, k, sc, rc, i).wait_send())
    each_peer(lambda i: band_copy(partial, final, True, band, sd, rd, i).wait_send())


def solution(mesh):
    small, fwd, inv01, inv2 = constants()
    vmem = pl.BlockSpec(memory_space=pltpu.VMEM)
    smem = pl.BlockSpec(memory_space=pltpu.SMEM)
    hbm = pl.BlockSpec(memory_space=pl.ANY)
    one = (N * BLK, LANES)
    two = (2 * N * BLK, LANES)
    sems = lambda n: pltpu.SemaphoreType.DMA((n,))

    def body(orbitals, partners, counts):
        forces, energy = pl.pallas_call(
            kernel,
            out_shape=(
                jax.ShapeDtypeStruct((3, N, NY * NZ), F32),
                jax.ShapeDtypeStruct((1, 1), F32),
            ),
            in_specs=[vmem, smem, smem, vmem, hbm, hbm, hbm],
            out_specs=(vmem, smem),
            scratch_shapes=[
                pltpu.VMEM(one, F32),
                pltpu.VMEM((N, BLK, LANES), F32),
                pltpu.VMEM(two, F32),
                pltpu.VMEM(two, F32),
                pltpu.VMEM(two, F32),
                pltpu.VMEM(two, F32),
                pltpu.VMEM(one, F32),
                pltpu.VMEM(one, F32),
                pltpu.VMEM(two, F32),
                pltpu.VMEM((BLK, LANES), F32),
                pltpu.VMEM(one, F32),
                pltpu.VMEM((BLK, LANES), F32),
                pltpu.VMEM((48 * 48, LANES), F32),
                pltpu.VMEM((48 * 48, LANES), F32),
                pltpu.VMEM(fwd.shape, BF16),
                pltpu.VMEM(inv01.shape, BF16),
                pltpu.VMEM(inv2.shape, BF16),
                sems(3),
                sems(N), sems(N),
                sems(2 * N), sems(2 * N),
                sems(2 * N), sems(2 * N),
                sems(N), sems(N),
                sems(N), sems(N),
            ],
            compiler_params=pltpu.CompilerParams(
                collective_id=0, has_side_effects=True, vmem_limit_bytes=48 * 1024 * 1024
            ),
        )(
            orbitals.transpose(1, 0, 2), partners.T, counts.T,
            jnp.asarray(small), jnp.asarray(fwd), jnp.asarray(inv01), jnp.asarray(inv2),
        )
        return forces.transpose(1, 0, 2), energy.reshape(())

    specs = P("band", "slab", None)
    return jax.shard_map(
        body, mesh=mesh, in_specs=(specs, P(), P()), out_specs=(specs, P()), check_vma=False
    )
```

time: 242 us -> 82.1 us (0.34)
  blocking collectives: 90.7 us -> 0 us
  Pallas kernels: 0 us -> 72.5 us
  waiting for transfers between devices: 52 us -> 0 us
  starting transfers between devices: 33.5 us -> 0 us
  local copies, waits for them, and re-layouts: 30.4 us -> 6.53 us
  matrix products: 21.5 us -> 0 us
  other arithmetic: 10.6 us -> 0 us
    pallas_call x0 -> x1, Pallas kernels: none -> 72.5 us  [body(): pl.pallas_call(kernel, out_shape=(jax.ShapeDtypeStruct((3, N, NY * NZ), F...]
    psum x5 -> x0, blocking collectives: 62.1 us -> none  [over_axes(): return functools.reduce(lax.psum, axes, value)]
    all_to_all x5 -> x0, waiting for transfers between devices: 52 us -> none  [the longest x1 21.4 us: body(): lax.all_to_all(wanted, BAND, split_axis=0, concat_axis=1, tiled=True)]
    all_to_all x5 -> x0, starting transfers between devices: 33.5 us -> none  [the longest x1 8.44 us: body(): lax.all_to_all(orbitals, SLAB, split_axis=0, concat_axis=1, tiled=True)]
    all_to_all x1 -> x0, blocking collectives: 28.6 us -> none  [body(): lax.all_to_all(outgoing, BAND, split_axis=1, concat_axis=0, tiled=True)]
    dot_general x7 -> x0, matrix products: 21.5 us -> none  [the longest x1 8.13 us: screened_potential(): jnp.einsum('coxyk,cdkz->doxyz', spectrum, dft_block(NZP, NZ, NZP, -1.0),...]
    reshape x4 -> x0, local copies, waits for them, and re-layouts: 11.4 us -> none  [the longest x3 9.42 us: body(): visitors = visitors.reshape((2, per_device) + own_orbs.shape[1:])]
    mul x6 -> x0, local copies, waits for them, and re-layouts: 4.8 us -> none  [the longest x2 2.26 us: pair_terms(): pair_density = own_orbs[None] * visitors * active[:, :, None, None]]
  transfers between devices with their start and end apart: 5 -> 0, of which waited for: 4 -> 0; matrix products, arithmetic and copies ran while one was open for 4% -> 0% of each run, Pallas kernels for 0% -> 0%
where the time goes in v1:
time: 82.1 us; the launch traced here: 81.4 us
  Pallas kernels  72.5 us (88%)
  local copies, waits for them, and re-layouts  6.53 us (8%)
  between operations  2.35 us (3%)
    pallas_call x1, Pallas kernels, body(): pl.pallas_call(kernel, out_shape=(jax.ShapeDtypeStruct((3, N, NY * NZ), F...  72.5 us
    unnamed x15, local copies, waits for them, and re-layouts  6.53 us

profile of v1, /device:TPU:1, one launch (start us, length us, event | category | flops | bytes accessed | tf_op | source)
XLA Modules:
  0.0 81.4 jit_solution(10281870809952509659)
XLA Ops:
  0.6 0.0 copy-start.6
  0.6 0.0 copy-start.5
  0.6 0.7 copy-done.6
  1.3 0.0 copy-done.5
  1.3 0.0 copy-start
  1.3 1.1 %copy-done = bf16[1536,256]{1,0:T(8,128)(2,1)S(1)} copy-done((bf16[1536,256]{1,0:T(8,128)(2,1)S(1)}, bf16[1536,256]{1,0:T(8,128)(2,1)}, u32[]{:S(2)}) %copy-start) | copy-done | bytes 786456
  2.5 0.0 copy-start.1
  2.5 1.1 %copy-done.1 = bf16[1536,256]{1,0:T(8,128)(2,1)S(1)} copy-done((bf16[1536,256]{1,0:T(8,128)(2,1)S(1)}, bf16[1536,256]{1,0:T(8,128)(2,1)}, u32[]{:S(2)}) %copy-start.1) | copy-done | bytes 786456
  3.6 0.0 copy-start.2
  3.6 1.0 %copy-done.2 = f32[16,3,2304]{2,0,1:T(8,128)S(1)} copy-done((f32[16,3,2304]{2,0,1:T(8,128)S(1)}, f32[16,3,2304]{2,0,1:T(8,128)}, u32[]{:S(2)}) %copy-start.2) | copy-done | bytes 442392
  4.6 0.0 copy-start.3
  4.6 0.9 %copy-done.3 = bf16[768,128]{1,0:T(8,128)(2,1)S(1)} copy-done((bf16[768,128]{1,0:T(8,128)(2,1)S(1)}, bf16[768,128]{1,0:T(8,128)(2,1)}, u32[]{:S(2)}) %copy-start.3) | copy-done | bytes 196632
  5.5 0.0 copy-start.4
  5.5 0.9 %copy-done.4 = bf16[3,48,144]{2,1,0:T(8,128)(2,1)S(1)} copy-done((bf16[3,48,144]{2,1,0:T(8,128)(2,1)S(1)}, bf16[3,48,144]{2,1,0:T(8,128)(2,1)}, u32[]{:S(2)}) %copy-start.4) | copy-done | bytes 41496
  6.4 72.5 %shard_map.86 = (f32[3,16,2304]{2,1,0:T(8,128)S(1)}, f32[1,1]{1,0:T(1,128)}) custom-call(f32[3,16,2304]{2,1,0:T(8,128)S(1)} %bitcast.6, s32[2,16]{1,0:T(2,128)S(1)} %bitcast.7, s32[2,16]{1,0:T(2,128)S(1)} %bitcast.8, bf16[3,48,144]{2,1,0:T(8,128)(2,1)S(1)} %copy-done.4, bf16[1536,256]{1,0:T(8,128)(2,1)S(1)} %copy-done.1, bf16[1536,256]{1,0:T(8,128)(2,1)S(1)} %copy-done, ...), custom_call_target="tpu_custom_call" | custom-call | tf_op jit(solution)/shard_map/pallas_call | solution.py:398
  78.9 0.8 copy.11
Async XLA Ops:
  0.6 0.7 copy-start.6
  0.6 0.7 copy-start.5
  1.3 1.1 %copy-start = (bf16[1536,256]{1,0:T(8,128)(2,1)S(1)}, bf16[1536,256]{1,0:T(8,128)(2,1)}, u32[]{:S(2)}) copy-start(bf16[1536,256]{1,0:T(8,128)(2,1)} %constant.10.clone.inv01_hbm) | copy-start | bytes 2359300
  2.5 1.1 %copy-start.1 = (bf16[1536,256]{1,0:T(8,128)(2,1)S(1)}, bf16[1536,256]{1,0:T(8,128)(2,1)}, u32[]{:S(2)}) copy-start(bf16[1536,256]{1,0:T(8,128)(2,1)} %constant.9.clone.fwd_hbm) | copy-start | bytes 2359300
  3.6 1.0 %copy-start.2 = (f32[16,3,2304]{2,0,1:T(8,128)S(1)}, f32[16,3,2304]{2,0,1:T(8,128)}, u32[]{:S(2)}) copy-start(f32[16,3,2304]{2,0,1:T(8,128)} %param.7) | copy-start | bytes 1327108
  4.6 0.9 %copy-start.3 = (bf16[768,128]{1,0:T(8,128)(2,1)S(1)}, bf16[768,128]{1,0:T(8,128)(2,1)}, u32[]{:S(2)}) copy-start(bf16[768,128]{1,0:T(8,128)(2,1)} %constant.11.clone.inv2_hbm) | copy-start | bytes 589828
  5.5 0.9 %copy-start.4 = (bf16[3,48,144]{2,1,0:T(8,128)(2,1)S(1)}, bf16[3,48,144]{2,1,0:T(8,128)(2,1)}, u32[]{:S(2)}) copy-start(bf16[3,48,144]{2,1,0:T(8,128)(2,1)} %constant.8.clone.small) | copy-start | bytes 124420

commit v2 on v1

--- a/solution.py
+++ b/solution.py
@@ -17,9 +17,11 @@
 ROWS = 54
 BLK = 56
 LANES = 128
+CHUNKS = ((0, 24), (24, 16), (40, 16))
 PAIRS = 2 * N
 SLATER = -((3.0 / math.pi) ** (1.0 / 3.0))
 MIX = 0.25
+VMEM_BYTES = 67_043_328
 SCREENING = 0.25
 F32 = jnp.float32
 BF16 = jnp.bfloat16
@@ -195,22 +197,36 @@
     pot[pl.ds(base + ROWS, 16, stride=BLK), :] = jnp.broadcast_to(total, (16, LANES))
 
 
+def rows_of(index, first, count):
+    return pl.ds(pl.multiple_of(index * BLK + first, 8), count)
+
+
 def block(index):
-    return pl.ds(pl.multiple_of(index * BLK, 8), BLK)
-
-
-def slot(ref, index):
-    return ref.at[index] if len(ref.shape) == 3 else ref.at[block(index)]
+    return rows_of(index, 0, BLK)
 
 
 def kernel(
-    orb, partners, counts, small, fwd_hbm, inv01_hbm, inv2_hbm,
+    orb_hbm, partners_hbm, counts_hbm, small_hbm, fwd_hbm, inv01_hbm, inv2_hbm,
     forces, energy_out,
-    src, held, pairs, tasks, pots, back, partial, final, ret, dens, dens_in, local, work, table, fwd, inv01, inv2,
-    const_sems, sa, ra, sb, rb, sc, rc, sd, rd, sn, rn,
+    orb, partners, counts, small, fwd, inv01, inv2,
+    src, held0, held1, held2, pairs, tasks, pots, back, partial, final, ret, dens, dens_in, local, work, table,
+    load_sems, sa, ra, sb, rb, sc, rc, sd, rd, sn, rn,
 ):
     band = lax.axis_index("band")
     slab = lax.axis_index("slab")
+    held = (held0, held1, held2)
+
+    loads = [
+        pltpu.make_async_copy(a, b, load_sems.at[i])
+        for i, (a, b) in enumerate(
+            (
+                (orb_hbm, orb), (partners_hbm, partners), (counts_hbm, counts),
+                (small_hbm, small), (fwd_hbm, fwd), (inv01_hbm, inv01), (inv2_hbm, inv2),
+            )
+        )
+    ]
+    for load in loads:
+        load.start()
 
     def peer(me, i):
         return lax.rem(me + i, N)
@@ -229,12 +245,7 @@
         pl.semaphore_signal(barrier, inc=1, device_id={"slab": peer(slab, i)}, device_id_type=MESH)
 
     each_peer(greet)
-    loads = [
-        pltpu.make_async_copy(a, b, const_sems.at[i])
-        for i, (a, b) in enumerate(((fwd_hbm, fwd), (inv01_hbm, inv01), (inv2_hbm, inv2)))
-    ]
-    for load in loads:
-        load.start()
+    loads[0].wait()
 
     for plane in range(3):
         for chunk in range(18):
@@ -243,80 +254,84 @@
             dens[pl.ds(plane * 18 + chunk, 1), :] = jnp.sum(tile * tile, axis=0, keepdims=True)
     pl.semaphore_wait(barrier, 2 * (N - 1))
 
-    def band_copy(a, b, at_peer, at_me, send, recv, i):
-        p = peer(band, i)
+    def remote(a, b, send, recv, axis, p):
         return pltpu.make_async_remote_copy(
-            src_ref=a.at[block(p)] if at_peer else a,
-            dst_ref=slot(b, at_me),
-            send_sem=send.at[p],
-            recv_sem=recv.at[at_me],
-            device_id={"band": p},
-            device_id_type=MESH,
-        )
-
-    def slab_copy(a, b, k, send, recv, i):
-        p = peer(slab, i)
-        return pltpu.make_async_remote_copy(
-            src_ref=a.at[block(k * N + p)],
-            dst_ref=b.at[block(k * N + slab)],
-            send_sem=send.at[k * N + p],
-            recv_sem=recv.at[k * N + slab],
-            device_id={"slab": p},
-            device_id_type=MESH,
-        )
-
-    def landed(b, k, at, recv, send, p):
-        return pltpu.make_async_remote_copy(
-            src_ref=slot(b, k * N + p),
-            dst_ref=slot(b, k * N + p),
-            send_sem=send.at[k * N + p],
-            recv_sem=recv.at[k * N + p],
-            device_id=at,
-            device_id_type=MESH,
-        )
-
-    def wait_band(b, recv, send):
-        each_peer(
-            lambda i: landed(b, 0, {"band": peer(band, i)}, recv, send, peer(band, i)).wait_recv()
-        )
-
-    def wait_slab(b, k, recv, send):
-        each_peer(
-            lambda i: landed(b, k, {"slab": peer(slab, i)}, recv, send, peer(slab, i)).wait_recv()
-        )
-
-    each_peer(lambda i: band_copy(src, held, True, band, sa, ra, i).start())
-    held[band] = src[block(band), :]
-    each_peer(lambda i: band_copy(dens, dens_in, False, band, sn, rn, i).start())
+            src_ref=a, dst_ref=b, send_sem=send, recv_sem=recv,
+            device_id={axis: p}, device_id_type=MESH,
+        )
+
+    def orbital_copy(c, p, at):
+        first, count = CHUNKS[c]
+        return remote(
+            src.at[rows_of(p, first, count)], held[c].at[at],
+            sa.at[c * N + p], ra.at[c * N + at], "band", p,
+        )
+
+    def square_copy(p, at):
+        return remote(dens, dens_in.at[block(at)], sn.at[p], rn.at[at], "band", p)
+
+    def pair_copy(k, c, p, at):
+        first, count = CHUNKS[c]
+        sem = (k * 3 + c) * N
+        return remote(
+            pairs.at[rows_of(k * N + p, first, count)], tasks.at[rows_of(k * N + at, first, count)],
+            sb.at[sem + p], rb.at[sem + at], "slab", p,
+        )
+
+    def pot_copy(k, c, p, at):
+        first, count = CHUNKS[c]
+        sem = (k * 3 + c) * N
+        return remote(
+            pots.at[rows_of(k * N + p, first, count)], back.at[rows_of(k * N + at, first, count)],
+            sc.at[sem + p], rc.at[sem + at], "slab", p,
+        )
+
+    def exchange_copy(c, p, at):
+        first, count = CHUNKS[c]
+        return remote(
+            partial.at[rows_of(p, first, count)], final.at[rows_of(at, first, count)],
+            sd.at[c * N + p], rd.at[c * N + at], "band", p,
+        )
+
+    for c in range(3):
+        each_peer(lambda i, c=c: orbital_copy(c, peer(band, i), band).start())
+    each_peer(lambda i: square_copy(peer(band, i), band).start())
+    for c, (first, count) in enumerate(CHUNKS):
+        held[c][band] = src[rows_of(band, first, count), :]
     dens_in[block(band), :] = dens[...]
 
     fill_table(table)
-    wait_band(held, ra, sa)
+    loads[1].wait()
+    loads[2].wait()
+
+    for c, (first, count) in enumerate(CHUNKS):
+        each_peer(lambda i, c=c: orbital_copy(c, peer(band, i), peer(band, i)).wait_recv())
+        for k in range(2):
+            def pair(g, k=k, c=c):
+                partner = partners[k, g]
+                active = jnp.where(band < counts[k, g], 1.0, 0.0).astype(F32)
+                return held[c][g] * held[c][partner] * active
+
+            def send_pair(i, k=k, c=c, first=first, count=count, pair=pair):
+                g = peer(slab, i)
+                pairs[rows_of(k * N + g, first, count), :] = pair(g)
+                pair_copy(k, c, g, slab).start()
+
+            each_peer(send_pair)
+            tasks[rows_of(k * N + slab, first, count), :] = pair(slab)
+
+    for load in loads[3:]:
+        load.wait()
 
     for k in range(2):
-        def pair(g, k=k):
-            partner = partners[k, g]
-            active = jnp.where(band < counts[k, g], 1.0, 0.0).astype(F32)
-            return held[g] * held[partner] * active
-
-        def send_pair(i, k=k):
-            g = peer(slab, i)
-            pairs[block(k * N + g), :] = pair(g)
-            slab_copy(pairs, tasks, k, sb, rb, i).start()
-
-        each_peer(send_pair)
-        tasks[block(k * N + slab), :] = pair(slab)
-
-    for load in loads:
-        load.wait()
-
-    for k in range(2):
-        wait_slab(tasks, k, rb, sb)
+        for c in range(3):
+            each_peer(lambda i, k=k, c=c: pair_copy(k, c, peer(slab, i), peer(slab, i)).wait_recv())
         convolve(tasks, pots, k * N * BLK, work, table, small, fwd, inv01, inv2)
-        each_peer(lambda i: slab_copy(pots, back, k, sc, rc, i).start())
+        for c in range(3):
+            each_peer(lambda i, k=k, c=c: pot_copy(k, c, peer(slab, i), slab).start())
         back[block(k * N + slab), :] = pots[block(k * N + slab), :]
 
-    wait_band(dens_in, rn, sn)
+    each_peer(lambda i: square_copy(peer(band, i), peer(band, i)).wait_recv())
     total = dens_in[pl.ds(0, BLK), :]
     for b in range(1, N):
         total = total + dens_in[pl.ds(b * BLK, BLK), :]
@@ -335,41 +350,41 @@
     onehot = jnp.where(names == row, 1.0, 0.0).astype(BF16)
     onehot3 = jnp.concatenate([onehot, onehot, onehot], axis=1)
 
-    wait_slab(back, 0, rc, sc)
-    wait_slab(back, 1, rc, sc)
-
-    def own_terms(g, carry):
-        phi = held[g]
-        own = jnp.zeros((BLK, LANES), F32)
+    for c, (first, count) in enumerate(CHUNKS):
         for k in range(2):
-            pot = back[block(k * N + g), :]
-            own = own + pot * held[partners[k, g]]
-            ret[block(k * N + g), :] = pot * phi
-        partial[block(g), :] = own
-        return carry
-
-    lax.fori_loop(0, N, own_terms, 0)
-
-    for first in range(0, ROWS, 9):
-        wide = jnp.concatenate(
-            [ret[pl.ds(first + u, PAIRS, stride=BLK), :] for u in range(9)], axis=1
-        )
-        hi, mid = split(wide)
-        low = (wide - hi.astype(F32) - mid.astype(F32)).astype(BF16)
-        summed = dot(onehot3, jnp.concatenate([hi, mid, low], axis=0))
-        for u in range(9):
-            at = pl.ds(first + u, N, stride=BLK)
-            partial[at, :] = -MIX * (partial[at, :] + summed[:, u * LANES : (u + 1) * LANES])
-    index_energy = jnp.sum(back[pl.ds(ROWS, PAIRS, stride=BLK), :], axis=0, keepdims=True)
-    partial[pl.ds(ROWS, N, stride=BLK), :] = jnp.broadcast_to(index_energy, (N, LANES))
-
-    each_peer(lambda i: band_copy(partial, final, True, band, sd, rd, i).start())
-    final[block(band), :] = partial[block(band), :]
-    wait_band(final, rd, sd)
-
-    for plane in range(3):
-        for chunk in range(18):
-            r = plane * 18 + chunk
+            each_peer(lambda i, k=k, c=c: pot_copy(k, c, peer(slab, i), peer(slab, i)).wait_recv())
+
+        def own_terms(g, carry, c=c, first=first, count=count):
+            phi = held[c][g]
+            own = jnp.zeros((count, LANES), F32)
+            for k in range(2):
+                pot = back[rows_of(k * N + g, first, count), :]
+                own = own + pot * held[c][partners[k, g]]
+                ret[rows_of(k * N + g, first, count), :] = pot * phi
+            partial[rows_of(g, first, count), :] = own
+            return carry
+
+        lax.fori_loop(0, N, own_terms, 0, unroll=2)
+        for eight in range(first, first + count, 8):
+            wide = jnp.concatenate(
+                [ret[pl.ds(eight + u, PAIRS, stride=BLK), :] for u in range(8)], axis=1
+            )
+            hi, mid = split(wide)
+            low = (wide - hi.astype(F32) - mid.astype(F32)).astype(BF16)
+            summed = dot(onehot3, jnp.concatenate([hi, mid, low], axis=0))
+            for u in range(min(8, ROWS - eight)):
+                at = pl.ds(eight + u, N, stride=BLK)
+                partial[at, :] = -MIX * (partial[at, :] + summed[:, u * LANES : (u + 1) * LANES])
+        if c == 2:
+            index_energy = jnp.sum(back[pl.ds(ROWS, PAIRS, stride=BLK), :], axis=0, keepdims=True)
+            partial[pl.ds(ROWS, N, stride=BLK), :] = jnp.broadcast_to(index_energy, (N, LANES))
+        each_peer(lambda i, c=c: exchange_copy(c, peer(band, i), band).start())
+        final[rows_of(band, first, count), :] = partial[rows_of(band, first, count), :]
+
+    for c, (first, count) in enumerate(CHUNKS):
+        each_peer(lambda i, c=c: exchange_copy(c, peer(band, i), peer(band, i)).wait_recv())
+        for r in range(first, min(ROWS, first + count)):
+            plane, chunk = divmod(r, 18)
             lanes = slice(chunk * LANES, (chunk + 1) * LANES)
             forces[plane, :, lanes] = (
                 local[pl.ds(r, 1), :] * orb[plane, :, lanes] + final[pl.ds(r, N, stride=BLK), :]
@@ -377,12 +392,13 @@
     energies = final[pl.ds(ROWS, N, stride=BLK), :]
     energy_out[0, 0] = jnp.sum(energies) * (-1.0 / (2.0 * N * N * NX * NY * NZ))
 
-    each_peer(lambda i: band_copy(src, held, True, band, sa, ra, i).wait_send())
-    each_peer(lambda i: band_copy(dens, dens_in, False, band, sn, rn, i).wait_send())
-    for k in range(2):
-        each_peer(lambda i: slab_copy(pairs, tasks, k, sb, rb, i).wait_send())
-        each_peer(lambda i: slab_copy(pots, back, k, sc, rc, i).wait_send())
-    each_peer(lambda i: band_copy(partial, final, True, band, sd, rd, i).wait_send())
+    each_peer(lambda i: square_copy(peer(band, i), band).wait_send())
+    for c in range(3):
+        each_peer(lambda i, c=c: orbital_copy(c, peer(band, i), band).wait_send())
+        each_peer(lambda i, c=c: exchange_copy(c, peer(band, i), band).wait_send())
+        for k in range(2):
+            each_peer(lambda i, k=k, c=c: pair_copy(k, c, peer(slab, i), slab).wait_send())
+            each_peer(lambda i, k=k, c=c: pot_copy(k, c, peer(slab, i), slab).wait_send())
 
 
 def solution(mesh):
@@ -390,8 +406,10 @@
     vmem = pl.BlockSpec(memory_space=pltpu.VMEM)
     smem = pl.BlockSpec(memory_space=pltpu.SMEM)
     hbm = pl.BlockSpec(memory_space=pl.ANY)
-    one = (N * BLK, LANES)
-    two = (2 * N * BLK, LANES)
+    one = pltpu.VMEM((N * BLK, LANES), F32)
+    two = pltpu.VMEM((2 * N * BLK, LANES), F32)
+    line = pltpu.VMEM((BLK, LANES), F32)
+    grid = pltpu.VMEM((48 * 48, LANES), F32)
     sems = lambda n: pltpu.SemaphoreType.DMA((n,))
 
     def body(orbitals, partners, counts):
@@ -401,35 +419,29 @@
                 jax.ShapeDtypeStruct((3, N, NY * NZ), F32),
                 jax.ShapeDtypeStruct((1, 1), F32),
             ),
-            in_specs=[vmem, smem, smem, vmem, hbm, hbm, hbm],
+            in_specs=[hbm] * 7,
             out_specs=(vmem, smem),
             scratch_shapes=[
-                pltpu.VMEM(one, F32),
-                pltpu.VMEM((N, BLK, LANES), F32),
-                pltpu.VMEM(two, F32),
-                pltpu.VMEM(two, F32),
-                pltpu.VMEM(two, F32),
-                pltpu.VMEM(two, F32),
-                pltpu.VMEM(one, F32),
-                pltpu.VMEM(one, F32),
-                pltpu.VMEM(two, F32),
-                pltpu.VMEM((BLK, LANES), F32),
-                pltpu.VMEM(one, F32),
-                pltpu.VMEM((BLK, LANES), F32),
-                pltpu.VMEM((48 * 48, LANES), F32),
-                pltpu.VMEM((48 * 48, LANES), F32),
-                pltpu.VMEM(fwd.shape, BF16),
-                pltpu.VMEM(inv01.shape, BF16),
-                pltpu.VMEM(inv2.shape, BF16),
-                sems(3),
-                sems(N), sems(N),
-                sems(2 * N), sems(2 * N),
-                sems(2 * N), sems(2 * N),
-                sems(N), sems(N),
+                pltpu.VMEM((3, N, NY * NZ), F32),
+                pltpu.SMEM((2, N), jnp.int32),
+                pltpu.SMEM((2, N), jnp.int32),
+                *[pltpu.VMEM(w.shape, BF16) for w in (small, fwd, inv01, inv2)],
+                one,
+                *[pltpu.VMEM((N, count, LANES), F32) for _, count in CHUNKS],
+                two, two, two, two,
+                one, one,
+                two,
+                line, one, line,
+                grid, grid,
+                sems(7),
+                sems(3 * N), sems(3 * N),
+                sems(6 * N), sems(6 * N),
+                sems(6 * N), sems(6 * N),
+                sems(3 * N), sems(3 * N),
                 sems(N), sems(N),
             ],
             compiler_params=pltpu.CompilerParams(
-                collective_id=0, has_side_effects=True, vmem_limit_bytes=48 * 1024 * 1024
+                collective_id=0, has_side_effects=True, vmem_limit_bytes=VMEM_BYTES
             ),
         )(
             orbitals.transpose(1, 0, 2), partners.T, counts.T,

time: 82.1 us -> 80.4 us (0.979)
  local copies, waits for them, and re-layouts: 6.53 us -> 1.8 us
  Pallas kernels: 72.5 us -> 76 us
    unnamed x15 -> x1, local copies, waits for them, and re-layouts: 6.53 us -> 1.8 us
    pallas_call x1, Pallas kernels: 72.5 us -> 76 us  [body(): pl.pallas_call(kernel, out_shape=(jax.ShapeDtypeStruct((3, N, NY * NZ), F...]
where the time goes in v2:
time: 80.4 us; the launch traced here: 80.3 us
  Pallas kernels  76 us (95%)
  between operations  2.44 us (3%)
  local copies, waits for them, and re-layouts  1.8 us (2%)
    pallas_call x1, Pallas kernels, body(): pl.pallas_call(kernel, out_shape=(jax.ShapeDtypeStruct((3, N, NY * NZ), F...  76 us
    unnamed x1, local copies, waits for them, and re-layouts  1.8 us

profile of v2, /device:TPU:1, one launch (start us, length us, event | category | flops | bytes accessed | tf_op | source)
XLA Modules:
  0.0 80.3 jit_solution(1945079149308553408)
XLA Ops:
  0.6 76.0 %shard_map.86 = (f32[3,16,2304]{2,1,0:T(8,128)}, f32[1,1]{1,0:T(1,128)}) custom-call(f32[3,16,2304]{2,1,0:T(8,128)} %bitcast.6, s32[2,16]{1,0:T(2,128)} %bitcast.7, s32[2,16]{1,0:T(2,128)} %bitcast.8, bf16[3,48,144]{2,1,0:T(8,128)(2,1)} %constant.8.clone.small_hbm, bf16[1536,256]{1,0:T(8,128)(2,1)} %constant.9.clone.fwd_hbm, ...), custom_call_target="tpu_custom_call" | custom-call | tf_op jit(solution)/shard_map/pallas_call | solution.py:416
  76.7 1.8 %copy.11 = f32[16,3,2304]{2,0,1:T(8,128)} copy(f32[16,3,2304]{2,0,1:T(8,128)} %bitcast.5) | data formatting | bytes 884736

commit v3 on v2

--- a/solution.py
+++ b/solution.py
@@ -17,11 +17,13 @@
 ROWS = 54
 BLK = 56
 LANES = 128
-CHUNKS = ((0, 24), (24, 16), (40, 16))
+CHUNKS = ((0, BLK),)
+PARTS = len(CHUNKS)
+TILES = BLK // 8
 PAIRS = 2 * N
 SLATER = -((3.0 / math.pi) ** (1.0 / 3.0))
 MIX = 0.25
-VMEM_BYTES = 67_043_328
+VMEM_BYTES = 65_600_000
 SCREENING = 0.25
 F32 = jnp.float32
 BF16 = jnp.bfloat16
@@ -61,7 +63,10 @@
     back = full.T
     inv01 = back[0 : 6 * 128, 0:256]
     inv2 = back[5 * 128 : 8 * 128, 256:384]
-    return small, np.concatenate(split_np(fwd)), np.concatenate(split_np(inv01)), np.concatenate(split_np(inv2))
+    small = np.pad(small.reshape(144, 144), ((0, 0), (0, 112)))
+    return np.concatenate(
+        [*split_np(fwd), *split_np(inv01), np.concatenate(split_np(inv2), axis=1), small]
+    )
 
 
 def split(x):
@@ -103,7 +108,7 @@
     lax.fori_loop(0, 48, step, 0)
 
 
-def convolve(pd, pot, base, work, table, small, fwd, inv01, inv2):
+def convolve(pd, pot, base, work, table, dft):
     rows = 288
 
     def gather(ref, t):
@@ -127,17 +132,17 @@
         return jnp.concatenate([hi, lo], axis=0)
 
     s0 = stack(0)
-    scatter_z(0, dot3(s0, fwd[0:128], fwd[768 : 768 + 128], rows))
+    scatter_z(0, dot3(s0, dft[0:128], dft[768 : 768 + 128], rows))
     s1 = stack(1)
     s01 = jnp.concatenate([s0, s1], axis=1)
-    scatter_z(1, dot3(s01, fwd[128:384], fwd[768 + 128 : 768 + 384], rows))
+    scatter_z(1, dot3(s01, dft[128:384], dft[768 + 128 : 768 + 384], rows))
     s2 = stack(2)
     s12 = jnp.concatenate([s1, s2], axis=1)
-    scatter_z(2, dot3(s12, fwd[384:640], fwd[768 + 384 : 768 + 640], rows))
-    scatter_z(3, dot3(s2, fwd[640:768], fwd[768 + 640 : 768 + 768], rows))
+    scatter_z(2, dot3(s12, dft[384:640], dft[768 + 384 : 768 + 640], rows))
+    scatter_z(3, dot3(s2, dft[640:768], dft[768 + 640 : 768 + 768], rows))
 
     def along_x(which):
-        w3 = small[which]
+        w3 = dft[3456 + 48 * which : 3504 + 48 * which, 0:144]
 
         def step(i, carry):
             start = pl.multiple_of(i * 384, 8)
@@ -149,10 +154,10 @@
             )
             return carry
 
-        lax.fori_loop(0, 6, step, 0)
+        lax.fori_loop(0, 6, step, 0, unroll=6)
 
     along_x(0)
-    wy3 = small[1]
+    wy3 = dft[3504:3552, 0:144]
 
     def y_step(i, carry):
         qx = i * 8
@@ -167,7 +172,7 @@
             work[pl.ds(qx + u, 48, stride=48), :] = out[:, LANES * u : LANES * (u + 1)]
         return carry
 
-    lax.fori_loop(0, 6, y_step, 0)
+    lax.fori_loop(0, 6, y_step, 0, unroll=6)
     along_x(2)
 
     def gather_y8(y8):
@@ -188,11 +193,11 @@
 
     parts = [gather_y8(y8) for y8 in range(6)]
     first = jnp.concatenate(parts, axis=1)
-    out = dot3(first, inv01[0:768], inv01[768:1536], rows)
+    out = dot3(first, dft[1536:2304], dft[2304:3072], rows)
     energy = scatter_t(0, out[:, 0:128], energy)
     energy = scatter_t(1, out[:, 128:256], energy)
     second = jnp.concatenate([parts[5], gather_y8(6), gather_y8(7)], axis=1)
-    energy = scatter_t(2, dot3(second, inv2[0:384], inv2[384:768], rows), energy)
+    energy = scatter_t(2, dot3(second, dft[3072:3456, 0:128], dft[3072:3456, 128:256], rows), energy)
     total = jnp.sum(energy, axis=0, keepdims=True)
     pot[pl.ds(base + ROWS, 16, stride=BLK), :] = jnp.broadcast_to(total, (16, LANES))
 
@@ -206,22 +211,21 @@
 
 
 def kernel(
-    orb_hbm, partners_hbm, counts_hbm, small_hbm, fwd_hbm, inv01_hbm, inv2_hbm,
+    orb_hbm, partners_hbm, counts_hbm, dft_hbm,
     forces, energy_out,
-    orb, partners, counts, small, fwd, inv01, inv2,
-    src, held0, held1, held2, pairs, tasks, pots, back, partial, final, ret, dens, dens_in, local, work, table,
-    load_sems, sa, ra, sb, rb, sc, rc, sd, rd, sn, rn,
+    orb, partners, counts, dft,
+    src, pairs, tasks, pots, back, partial, final, ret, dens, dens_in, dens_tile, dens_all, local, work, table,
+    load_sems, sa, ra, sb, rb, sc, rc, sd, rd, sn, rn, st, rt, *held,
 ):
     band = lax.axis_index("band")
     slab = lax.axis_index("slab")
-    held = (held0, held1, held2)
 
     loads = [
         pltpu.make_async_copy(a, b, load_sems.at[i])
         for i, (a, b) in enumerate(
             (
                 (orb_hbm, orb), (partners_hbm, partners), (counts_hbm, counts),
-                (small_hbm, small), (fwd_hbm, fwd), (inv01_hbm, inv01), (inv2_hbm, inv2),
+                (dft_hbm, dft),
             )
         )
     ]
@@ -267,12 +271,21 @@
             sa.at[c * N + p], ra.at[c * N + at], "band", p,
         )
 
-    def square_copy(p, at):
-        return remote(dens, dens_in.at[block(at)], sn.at[p], rn.at[at], "band", p)
+    def tile_of(index):
+        return pl.ds(pl.multiple_of(index * 8, 8), 8)
+
+    def square_copy(p, tile, at):
+        return remote(dens.at[tile_of(tile)], dens_in.at[tile_of(at)], sn.at[p], rn.at[at], "band", p)
+
+    def density_copy(p, tile):
+        return remote(dens_tile, dens_all.at[tile_of(tile)], st.at[p], rt.at[tile], "band", p)
+
+    def if_summing(index, fn):
+        pl.when(index < TILES)(fn)
 
     def pair_copy(k, c, p, at):
         first, count = CHUNKS[c]
-        sem = (k * 3 + c) * N
+        sem = (k * PARTS + c) * N
         return remote(
             pairs.at[rows_of(k * N + p, first, count)], tasks.at[rows_of(k * N + at, first, count)],
             sb.at[sem + p], rb.at[sem + at], "slab", p,
@@ -280,7 +293,7 @@
 
     def pot_copy(k, c, p, at):
         first, count = CHUNKS[c]
-        sem = (k * 3 + c) * N
+        sem = (k * PARTS + c) * N
         return remote(
             pots.at[rows_of(k * N + p, first, count)], back.at[rows_of(k * N + at, first, count)],
             sc.at[sem + p], rc.at[sem + at], "slab", p,
@@ -293,12 +306,20 @@
             sd.at[c * N + p], rd.at[c * N + at], "band", p,
         )
 
-    for c in range(3):
+    for c in range(PARTS):
         each_peer(lambda i, c=c: orbital_copy(c, peer(band, i), band).start())
-    each_peer(lambda i: square_copy(peer(band, i), band).start())
     for c, (first, count) in enumerate(CHUNKS):
         held[c][band] = src[rows_of(band, first, count), :]
-    dens_in[block(band), :] = dens[...]
+
+    def to_summing(i):
+        p = peer(band, i)
+        if_summing(p, lambda: square_copy(p, p, band).start())
+
+    each_peer(to_summing)
+
+    @pl.when(band < TILES)
+    def _():
+        dens_in[tile_of(band), :] = dens[tile_of(band), :]
 
     fill_table(table)
     loads[1].wait()
@@ -306,35 +327,44 @@
 
     for c, (first, count) in enumerate(CHUNKS):
         each_peer(lambda i, c=c: orbital_copy(c, peer(band, i), peer(band, i)).wait_recv())
+        for g in range(N):
+            mine = held[c][g]
+            for k in range(2):
+                active = jnp.where(band < counts[k, g], 1.0, 0.0).astype(F32)
+                product = mine * held[c][partners[k, g]] * active
+                pairs[pl.ds((k * N + g) * BLK + first, count), :] = product
         for k in range(2):
-            def pair(g, k=k, c=c):
-                partner = partners[k, g]
-                active = jnp.where(band < counts[k, g], 1.0, 0.0).astype(F32)
-                return held[c][g] * held[c][partner] * active
-
-            def send_pair(i, k=k, c=c, first=first, count=count, pair=pair):
-                g = peer(slab, i)
-                pairs[rows_of(k * N + g, first, count), :] = pair(g)
-                pair_copy(k, c, g, slab).start()
-
-            each_peer(send_pair)
-            tasks[rows_of(k * N + slab, first, count), :] = pair(slab)
+            each_peer(lambda i, k=k, c=c: pair_copy(k, c, peer(slab, i), slab).start())
+            at = rows_of(k * N + slab, first, count)
+            tasks[at, :] = pairs[at, :]
+
+    @pl.when(band < TILES)
+    def _():
+        each_peer(lambda i: square_copy(peer(band, i), band, peer(band, i)).wait_recv())
+        summed = dens_in[0:8, :]
+        for b in range(1, N):
+            summed = summed + dens_in[b * 8 : (b + 1) * 8, :]
+        dens_tile[...] = summed
+        dens_all[tile_of(band), :] = summed
+        each_peer(lambda i: density_copy(peer(band, i), band).start())
 
     for load in loads[3:]:
         load.wait()
 
     for k in range(2):
-        for c in range(3):
+        for c in range(PARTS):
             each_peer(lambda i, k=k, c=c: pair_copy(k, c, peer(slab, i), peer(slab, i)).wait_recv())
-        convolve(tasks, pots, k * N * BLK, work, table, small, fwd, inv01, inv2)
-        for c in range(3):
+        convolve(tasks, pots, k * N * BLK, work, table, dft)
+        for c in range(PARTS):
             each_peer(lambda i, k=k, c=c: pot_copy(k, c, peer(slab, i), slab).start())
         back[block(k * N + slab), :] = pots[block(k * N + slab), :]
 
-    each_peer(lambda i: square_copy(peer(band, i), peer(band, i)).wait_recv())
-    total = dens_in[pl.ds(0, BLK), :]
-    for b in range(1, N):
-        total = total + dens_in[pl.ds(b * BLK, BLK), :]
+    def from_summing(i):
+        p = peer(band, i)
+        if_summing(p, lambda: density_copy(p, p).wait_recv())
+
+    each_peer(from_summing)
+    total = dens_all[...]
     total = total * (2.0 / (N * N))
     safe = jnp.maximum(total, 1e-37)
     root = jnp.exp(jnp.log(safe) * (1.0 / 3.0))
@@ -354,17 +384,15 @@
         for k in range(2):
             each_peer(lambda i, k=k, c=c: pot_copy(k, c, peer(slab, i), peer(slab, i)).wait_recv())
 
-        def own_terms(g, carry, c=c, first=first, count=count):
+        for g in range(N):
             phi = held[c][g]
             own = jnp.zeros((count, LANES), F32)
             for k in range(2):
-                pot = back[rows_of(k * N + g, first, count), :]
+                at = pl.ds((k * N + g) * BLK + first, count)
+                pot = back[at, :]
                 own = own + pot * held[c][partners[k, g]]
-                ret[rows_of(k * N + g, first, count), :] = pot * phi
-            partial[rows_of(g, first, count), :] = own
-            return carry
-
-        lax.fori_loop(0, N, own_terms, 0, unroll=2)
+                ret[at, :] = pot * phi
+            partial[pl.ds(g * BLK + first, count), :] = own
         for eight in range(first, first + count, 8):
             wide = jnp.concatenate(
                 [ret[pl.ds(eight + u, PAIRS, stride=BLK), :] for u in range(8)], axis=1
@@ -375,11 +403,23 @@
             for u in range(min(8, ROWS - eight)):
                 at = pl.ds(eight + u, N, stride=BLK)
                 partial[at, :] = -MIX * (partial[at, :] + summed[:, u * LANES : (u + 1) * LANES])
-        if c == 2:
+        if c == PARTS - 1:
             index_energy = jnp.sum(back[pl.ds(ROWS, PAIRS, stride=BLK), :], axis=0, keepdims=True)
             partial[pl.ds(ROWS, N, stride=BLK), :] = jnp.broadcast_to(index_energy, (N, LANES))
         each_peer(lambda i, c=c: exchange_copy(c, peer(band, i), band).start())
         final[rows_of(band, first, count), :] = partial[rows_of(band, first, count), :]
+
+    def summing_left(i):
+        p = peer(band, i)
+        if_summing(p, lambda: square_copy(p, p, band).wait_send())
+
+    each_peer(summing_left)
+    if_summing(band, lambda: each_peer(lambda i: density_copy(peer(band, i), band).wait_send()))
+    for c in range(PARTS):
+        each_peer(lambda i, c=c: orbital_copy(c, peer(band, i), band).wait_send())
+        for k in range(2):
+            each_peer(lambda i, k=k, c=c: pair_copy(k, c, peer(slab, i), slab).wait_send())
+            each_peer(lambda i, k=k, c=c: pot_copy(k, c, peer(slab, i), slab).wait_send())
 
     for c, (first, count) in enumerate(CHUNKS):
         each_peer(lambda i, c=c: exchange_copy(c, peer(band, i), peer(band, i)).wait_recv())
@@ -391,18 +431,12 @@
             )
     energies = final[pl.ds(ROWS, N, stride=BLK), :]
     energy_out[0, 0] = jnp.sum(energies) * (-1.0 / (2.0 * N * N * NX * NY * NZ))
-
-    each_peer(lambda i: square_copy(peer(band, i), band).wait_send())
-    for c in range(3):
-        each_peer(lambda i, c=c: orbital_copy(c, peer(band, i), band).wait_send())
+    for c in range(PARTS):
         each_peer(lambda i, c=c: exchange_copy(c, peer(band, i), band).wait_send())
-        for k in range(2):
-            each_peer(lambda i, k=k, c=c: pair_copy(k, c, peer(slab, i), slab).wait_send())
-            each_peer(lambda i, k=k, c=c: pot_copy(k, c, peer(slab, i), slab).wait_send())
 
 
 def solution(mesh):
-    small, fwd, inv01, inv2 = constants()
+    dft = constants()
     vmem = pl.BlockSpec(memory_space=pltpu.VMEM)
     smem = pl.BlockSpec(memory_space=pltpu.SMEM)
     hbm = pl.BlockSpec(memory_space=pl.ANY)
@@ -419,33 +453,35 @@
                 jax.ShapeDtypeStruct((3, N, NY * NZ), F32),
                 jax.ShapeDtypeStruct((1, 1), F32),
             ),
-            in_specs=[hbm] * 7,
+            in_specs=[hbm] * 4,
             out_specs=(vmem, smem),
             scratch_shapes=[
                 pltpu.VMEM((3, N, NY * NZ), F32),
                 pltpu.SMEM((2, N), jnp.int32),
                 pltpu.SMEM((2, N), jnp.int32),
-                *[pltpu.VMEM(w.shape, BF16) for w in (small, fwd, inv01, inv2)],
+                pltpu.VMEM(dft.shape, BF16),
                 one,
-                *[pltpu.VMEM((N, count, LANES), F32) for _, count in CHUNKS],
                 two, two, two, two,
                 one, one,
                 two,
-                line, one, line,
+                line, pltpu.VMEM((N * 8, LANES), F32),
+                pltpu.VMEM((8, LANES), F32), line, line,
                 grid, grid,
-                sems(7),
-                sems(3 * N), sems(3 * N),
-                sems(6 * N), sems(6 * N),
-                sems(6 * N), sems(6 * N),
-                sems(3 * N), sems(3 * N),
+                sems(4),
+                sems(PARTS * N), sems(PARTS * N),
+                sems(2 * PARTS * N), sems(2 * PARTS * N),
+                sems(2 * PARTS * N), sems(2 * PARTS * N),
+                sems(PARTS * N), sems(PARTS * N),
                 sems(N), sems(N),
+                sems(N), sems(N),
+                *[pltpu.VMEM((N, count, LANES), F32) for _, count in CHUNKS],
             ],
             compiler_params=pltpu.CompilerParams(
                 collective_id=0, has_side_effects=True, vmem_limit_bytes=VMEM_BYTES
             ),
         )(
             orbitals.transpose(1, 0, 2), partners.T, counts.T,
-            jnp.asarray(small), jnp.asarray(fwd), jnp.asarray(inv01), jnp.asarray(inv2),
+            jnp.asarray(dft),
         )
         return forces.transpose(1, 0, 2), energy.reshape(())
 

time: 80.4 us -> 69.5 us (0.86)
  Pallas kernels: 76 us -> 65.1 us
    pallas_call x1, Pallas kernels: 76 us -> 65.1 us  [body(): pl.pallas_call(kernel, out_shape=(jax.ShapeDtypeStruct((3, N, NY * NZ), F...]
where the time goes in v3:
time: 69.5 us; the launch traced here: 69.4 us
  Pallas kernels  65.1 us (94%)
  between operations  2.44 us (4%)
  local copies, waits for them, and re-layouts  1.8 us (3%)
    pallas_call x1, Pallas kernels, body(): pl.pallas_call(kernel, out_shape=(jax.ShapeDtypeStruct((3, N, NY * NZ), F...  65.1 us
    unnamed x1, local copies, waits for them, and re-layouts  1.8 us

profile of v3, /device:TPU:1, one launch (start us, length us, event | category | flops | bytes accessed | tf_op | source)
XLA Modules:
  0.0 69.4 jit_solution(11731508088791230661)
XLA Ops:
  0.6 65.1 %shard_map.59 = (f32[3,16,2304]{2,1,0:T(8,128)}, f32[1,1]{1,0:T(1,128)}) custom-call(f32[3,16,2304]{2,1,0:T(8,128)} %bitcast.6, s32[2,16]{1,0:T(2,128)} %bitcast.7, s32[2,16]{1,0:T(2,128)} %bitcast.8, bf16[3600,256]{1,0:T(8,128)(2,1)} %constant.2.clone.dft_hbm), custom_call_target="tpu_custom_call" | custom-call | tf_op jit(solution)/shard_map/pallas_call | solution.py:450
  65.7 1.8 %copy.8 = f32[16,3,2304]{2,0,1:T(8,128)} copy(f32[16,3,2304]{2,0,1:T(8,128)} %bitcast.5) | data formatting | bytes 884736

commit v4 on v3

--- a/solution.py
+++ b/solution.py
@@ -23,7 +23,7 @@
 PAIRS = 2 * N
 SLATER = -((3.0 / math.pi) ** (1.0 / 3.0))
 MIX = 0.25
-VMEM_BYTES = 65_600_000
+VMEM_BYTES = 56_000_000
 SCREENING = 0.25
 F32 = jnp.float32
 BF16 = jnp.bfloat16
@@ -233,7 +233,16 @@
         load.start()
 
     def peer(me, i):
-        return lax.rem(me + i, N)
+        j = i - 1
+        if me is band:
+            h = j // 2
+            dz = 4 + lax.rem(h, 2) * -((h + 1) // 2) + (1 - lax.rem(h, 2)) * (h // 2)
+            bx = lax.rem(band // 8 + 1 - lax.rem(j, 2), 2)
+            return bx * 8 + lax.rem(lax.rem(band, 8) + dz, 8)
+        h = j // 4
+        dy = jnp.where(h == 0, 2, jnp.where(h == 1, 1, jnp.where(h == 2, 3, 0)))
+        low = lax.bitwise_xor(lax.rem(slab, 4), 3 - lax.rem(j, 4))
+        return lax.rem(slab // 4 + dy, 4) * 4 + low
 
     def each_peer(fn):
         def step(i, carry):
@@ -334,7 +343,8 @@
                 product = mine * held[c][partners[k, g]] * active
                 pairs[pl.ds((k * N + g) * BLK + first, count), :] = product
         for k in range(2):
-            each_peer(lambda i, k=k, c=c: pair_copy(k, c, peer(slab, i), slab).start())
+            if k == 0:
+                each_peer(lambda i, k=k, c=c: pair_copy(k, c, peer(slab, i), slab).start())
             at = rows_of(k * N + slab, first, count)
             tasks[at, :] = pairs[at, :]
 
@@ -353,7 +363,13 @@
 
     for k in range(2):
         for c in range(PARTS):
-            each_peer(lambda i, k=k, c=c: pair_copy(k, c, peer(slab, i), peer(slab, i)).wait_recv())
+            def pair_in(i, k=k, c=c):
+                p = peer(slab, i)
+                pair_copy(k, c, p, p).wait_recv()
+                if k == 0:
+                    pair_copy(1, c, p, slab).start()
+
+            each_peer(pair_in)
         convolve(tasks, pots, k * N * BLK, work, table, dft)
         for c in range(PARTS):
             each_peer(lambda i, k=k, c=c: pot_copy(k, c, peer(slab, i), slab).start())

time: 69.5 us -> 67.7 us (0.974)
  Pallas kernels: 65.1 us -> 63 us
    pallas_call x1, Pallas kernels: 65.1 us -> 63 us  [body(): pl.pallas_call(kernel, out_shape=(jax.ShapeDtypeStruct((3, N, NY * NZ), F...]
    unnamed x1 -> x5, local copies, waits for them, and re-layouts: 1.8 us -> 2.12 us
where the time goes in v4:
time: 67.7 us; the launch traced here: 67.5 us
  Pallas kernels  63 us (93%)
  between operations  2.41 us (4%)
  local copies, waits for them, and re-layouts  2.12 us (3%)
    pallas_call x1, Pallas kernels, body(): pl.pallas_call(kernel, out_shape=(jax.ShapeDtypeStruct((3, N, NY * NZ), F...  63 us
    unnamed x5, local copies, waits for them, and re-layouts  2.12 us

profile of v4, /device:TPU:1, one launch (start us, length us, event | category | flops | bytes accessed | tf_op | source)
XLA Modules:
  0.0 67.5 jit_solution(15771408540874214218)
XLA Ops:
  0.6 0.0 copy-start
  0.6 0.7 copy-done
  1.3 0.0 copy-start.1
  1.3 0.7 %copy-done.1 = s32[16,2]{0,1:T(2,128)S(1)} copy-done((s32[16,2]{0,1:T(2,128)S(1)}, s32[16,2]{0,1:T(2,128)}, u32[]{:S(2)}) %copy-start.1) | copy-done | bytes 152
  2.0 63.0 %shard_map.59 = (f32[3,16,2304]{2,1,0:T(8,128)S(1)}, f32[1,1]{1,0:T(1,128)}) custom-call(f32[3,16,2304]{2,1,0:T(8,128)} %bitcast.8, s32[2,16]{1,0:T(2,128)S(1)} %bitcast.6, s32[2,16]{1,0:T(2,128)S(1)} %bitcast.7, bf16[3600,256]{1,0:T(8,128)(2,1)} %constant.2.clone.dft_hbm), custom_call_target="tpu_custom_call" | custom-call | tf_op jit(solution)/shard_map/pallas_call | solution.py:466
  65.0 0.8 %copy.8 = f32[16,3,2304]{2,0,1:T(8,128)} copy(f32[16,3,2304]{2,0,1:T(8,128)S(1)} %bitcast.5) | data formatting | bytes 884736
Async XLA Ops:
  0.6 0.7 %copy-start = (s32[16,2]{0,1:T(2,128)S(1)}, s32[16,2]{0,1:T(2,128)}, u32[]{:S(2)}) copy-start(s32[16,2]{0,1:T(2,128)} %param.5) | copy-start | bytes 388
  1.3 0.7 %copy-start.1 = (s32[16,2]{0,1:T(2,128)S(1)}, s32[16,2]{0,1:T(2,128)}, u32[]{:S(2)}) copy-start(s32[16,2]{0,1:T(2,128)} %param.6) | copy-start | bytes 388

commit v5 on v4

--- a/solution.py
+++ b/solution.py
@@ -387,38 +387,37 @@
     root = root * (2.0 + safe / (root * root * root)) * (1.0 / 3.0)
     local[...] = SLATER * jnp.where(total > 0.0, root, 0.0)
 
-    row = lax.broadcasted_iota(jnp.int32, (N, PAIRS), 0)
-    col = lax.broadcasted_iota(jnp.int32, (N, PAIRS), 1)
-    names = jnp.full((N, PAIRS), -1, jnp.int32)
+    row = lax.broadcasted_iota(jnp.int32, (N, N), 0)
+    col = lax.broadcasted_iota(jnp.int32, (N, N), 1)
+    onehots = []
     for k in range(2):
+        names = jnp.full((N, N), -1, jnp.int32)
         for g in range(N):
-            names = jnp.where(col == k * N + g, partners[k, g], names)
-    onehot = jnp.where(names == row, 1.0, 0.0).astype(BF16)
-    onehot3 = jnp.concatenate([onehot, onehot, onehot], axis=1)
+            names = jnp.where(col == g, partners[k, g], names)
+        onehot = jnp.where(names == row, 1.0, 0.0).astype(BF16)
+        onehots.append(jnp.concatenate([onehot, onehot, onehot], axis=1))
 
     for c, (first, count) in enumerate(CHUNKS):
         for k in range(2):
             each_peer(lambda i, k=k, c=c: pot_copy(k, c, peer(slab, i), peer(slab, i)).wait_recv())
-
-        for g in range(N):
-            phi = held[c][g]
-            own = jnp.zeros((count, LANES), F32)
-            for k in range(2):
+            for g in range(N):
                 at = pl.ds((k * N + g) * BLK + first, count)
+                to = pl.ds(g * BLK + first, count)
                 pot = back[at, :]
-                own = own + pot * held[c][partners[k, g]]
-                ret[at, :] = pot * phi
-            partial[pl.ds(g * BLK + first, count), :] = own
-        for eight in range(first, first + count, 8):
-            wide = jnp.concatenate(
-                [ret[pl.ds(eight + u, PAIRS, stride=BLK), :] for u in range(8)], axis=1
-            )
-            hi, mid = split(wide)
-            low = (wide - hi.astype(F32) - mid.astype(F32)).astype(BF16)
-            summed = dot(onehot3, jnp.concatenate([hi, mid, low], axis=0))
-            for u in range(min(8, ROWS - eight)):
-                at = pl.ds(eight + u, N, stride=BLK)
-                partial[at, :] = -MIX * (partial[at, :] + summed[:, u * LANES : (u + 1) * LANES])
+                own = pot * held[c][partners[k, g]]
+                ret[at, :] = pot * held[c][g]
+                partial[to, :] = own if k == 0 else partial[to, :] + own
+            for eight in range(first, first + count, 8):
+                wide = jnp.concatenate(
+                    [ret[pl.ds(k * N * BLK + eight + u, N, stride=BLK), :] for u in range(8)], axis=1
+                )
+                hi, mid = split(wide)
+                low = (wide - hi.astype(F32) - mid.astype(F32)).astype(BF16)
+                summed = dot(onehots[k], jnp.concatenate([hi, mid, low], axis=0))
+                for u in range(min(8, ROWS - eight)):
+                    at = pl.ds(eight + u, N, stride=BLK)
+                    value = partial[at, :] + summed[:, u * LANES : (u + 1) * LANES]
+                    partial[at, :] = value if k == 0 else -MIX * value
         if c == PARTS - 1:
             index_energy = jnp.sum(back[pl.ds(ROWS, PAIRS, stride=BLK), :], axis=0, keepdims=True)
             partial[pl.ds(ROWS, N, stride=BLK), :] = jnp.broadcast_to(index_energy, (N, LANES))

time: 67.7 us -> 67.5 us (level)
  no operation moved by 1% of the time
where the time goes in v5:
time: 67.5 us; the launch traced here: 67.3 us
  Pallas kernels  62.8 us (93%)
  between operations  2.41 us (4%)
  local copies, waits for them, and re-layouts  2.12 us (3%)
    pallas_call x1, Pallas kernels, body(): pl.pallas_call(kernel, out_shape=(jax.ShapeDtypeStruct((3, N, NY * NZ), F...  62.8 us
    unnamed x5, local copies, waits for them, and re-layouts  2.12 us

profile of v5, /device:TPU:1, one launch (start us, length us, event | category | flops | bytes accessed | tf_op | source)
XLA Modules:
  0.0 67.3 jit_solution(712602272881843412)
XLA Ops:
  0.6 0.0 copy-start
  0.6 0.7 copy-done
  1.3 0.0 copy-start.1
  1.3 0.7 %copy-done.1 = s32[16,2]{0,1:T(2,128)S(1)} copy-done((s32[16,2]{0,1:T(2,128)S(1)}, s32[16,2]{0,1:T(2,128)}, u32[]{:S(2)}) %copy-start.1) | copy-done | bytes 152
  2.0 62.8 %shard_map.59 = (f32[3,16,2304]{2,1,0:T(8,128)S(1)}, f32[1,1]{1,0:T(1,128)}) custom-call(f32[3,16,2304]{2,1,0:T(8,128)} %bitcast.8, s32[2,16]{1,0:T(2,128)S(1)} %bitcast.6, s32[2,16]{1,0:T(2,128)S(1)} %bitcast.7, bf16[3600,256]{1,0:T(8,128)(2,1)} %constant.2.clone.dft_hbm), custom_call_target="tpu_custom_call" | custom-call | tf_op jit(solution)/shard_map/pallas_call | solution.py:465
  64.8 0.8 %copy.8 = f32[16,3,2304]{2,0,1:T(8,128)} copy(f32[16,3,2304]{2,0,1:T(8,128)S(1)} %bitcast.5) | data formatting | bytes 884736
Async XLA Ops:
  0.6 0.7 %copy-start = (s32[16,2]{0,1:T(2,128)S(1)}, s32[16,2]{0,1:T(2,128)}, u32[]{:S(2)}) copy-start(s32[16,2]{0,1:T(2,128)} %param.5) | copy-start | bytes 388
  1.3 0.7 %copy-start.1 = (s32[16,2]{0,1:T(2,128)S(1)}, s32[16,2]{0,1:T(2,128)}, u32[]{:S(2)}) copy-start(s32[16,2]{0,1:T(2,128)} %param.6) | copy-start | bytes 388

commit v6 on v5

--- a/solution.py
+++ b/solution.py
@@ -264,7 +264,6 @@
         for chunk in range(18):
             tile = orb[plane, :, chunk * LANES : (chunk + 1) * LANES]
             src[pl.ds(plane * 18 + chunk, N, stride=BLK), :] = tile
-            dens[pl.ds(plane * 18 + chunk, 1), :] = jnp.sum(tile * tile, axis=0, keepdims=True)
     pl.semaphore_wait(barrier, 2 * (N - 1))
 
     def remote(a, b, send, recv, axis, p):
@@ -319,6 +318,10 @@
         each_peer(lambda i, c=c: orbital_copy(c, peer(band, i), band).start())
     for c, (first, count) in enumerate(CHUNKS):
         held[c][band] = src[rows_of(band, first, count), :]
+    for plane in range(3):
+        for chunk in range(18):
+            tile = orb[plane, :, chunk * LANES : (chunk + 1) * LANES]
+            dens[pl.ds(plane * 18 + chunk, 1), :] = jnp.sum(tile * tile, axis=0, keepdims=True)
 
     def to_summing(i):
         p = peer(band, i)

time: 67.5 us -> 67.5 us (level)
  no operation moved by 1% of the time
where the time goes in v6:
time: 67.5 us; the launch traced here: 67.3 us
  Pallas kernels  62.8 us (93%)
  between operations  2.41 us (4%)
  local copies, waits for them, and re-layouts  2.12 us (3%)
    pallas_call x1, Pallas kernels, body(): pl.pallas_call(kernel, out_shape=(jax.ShapeDtypeStruct((3, N, NY * NZ), F...  62.8 us
    unnamed x5, local copies, waits for them, and re-layouts  2.12 us

profile of v6, /device:TPU:1, one launch (start us, length us, event | category | flops | bytes accessed | tf_op | source)
XLA Modules:
  0.0 67.3 jit_solution(1676941240976885124)
XLA Ops:
  0.6 0.0 copy-start
  0.6 0.7 copy-done
  1.3 0.0 copy-start.1
  1.3 0.7 %copy-done.1 = s32[16,2]{0,1:T(2,128)S(1)} copy-done((s32[16,2]{0,1:T(2,128)S(1)}, s32[16,2]{0,1:T(2,128)}, u32[]{:S(2)}) %copy-start.1) | copy-done | bytes 152
  2.0 62.8 %shard_map.59 = (f32[3,16,2304]{2,1,0:T(8,128)S(1)}, f32[1,1]{1,0:T(1,128)}) custom-call(f32[3,16,2304]{2,1,0:T(8,128)} %bitcast.8, s32[2,16]{1,0:T(2,128)S(1)} %bitcast.6, s32[2,16]{1,0:T(2,128)S(1)} %bitcast.7, bf16[3600,256]{1,0:T(8,128)(2,1)} %constant.2.clone.dft_hbm), custom_call_target="tpu_custom_call" | custom-call | tf_op jit(solution)/shard_map/pallas_call | solution.py:468
  64.8 0.8 %copy.8 = f32[16,3,2304]{2,0,1:T(8,128)} copy(f32[16,3,2304]{2,0,1:T(8,128)S(1)} %bitcast.5) | data formatting | bytes 884736
Async XLA Ops:
  0.6 0.7 %copy-start = (s32[16,2]{0,1:T(2,128)S(1)}, s32[16,2]{0,1:T(2,128)}, u32[]{:S(2)}) copy-start(s32[16,2]{0,1:T(2,128)} %param.5) | copy-start | bytes 388
  1.3 0.7 %copy-start.1 = (s32[16,2]{0,1:T(2,128)S(1)}, s32[16,2]{0,1:T(2,128)}, u32[]{:S(2)}) copy-start(s32[16,2]{0,1:T(2,128)} %param.6) | copy-start | bytes 388
